TPU v7x, 512 devices: a whole 4x8x8 slice. The times are simulated.
512 devices in a mesh: head: 8 (over y_hi, core), blk: 64 (over z, y_lo, x).
Axes of the slice: x: 4, y: 8 (y_hi: 4, y_lo: 2; y = y_hi * 2 + y_lo), z: 8, core: 2. Of those that a mesh axis runs over, the one named last changes fastest.
Arguments:
- query_rows: bfloat16 [64, 144, 3072], P('blk', 'head'), may hold values from -6 to 6
- key_rows: bfloat16 [64, 144, 3072], P('blk', 'head'), may hold values from -6 to 6
- value_rows: bfloat16 [64, 144, 3072], P('blk', 'head'), may hold values from -6 to 6
- query_tangent: bfloat16 [64, 144, 3072], P('blk', 'head'), may hold values from -6 to 6
- key_tangent: bfloat16 [64, 144, 3072], P('blk', 'head'), may hold values from -6 to 6
- value_tangent: bfloat16 [64, 144, 3072], P('blk', 'head'), may hold values from -6 to 6
- query_gain: float32 [128], replicated, may hold values from 1 to 6
- key_gain: float32 [128], replicated, may hold values from 1 to 6
Outputs:
- attended: bfloat16 [64, 144, 3072], P('blk', 'head')
- attended_tangent: bfloat16 [64, 144, 3072], P('blk', 'head')
All inputs are finite; a program needn't handle non-finite values.
Results may differ from a plain program's by a relative error of at most 0.014.
The roundings to bfloat16 on the way count: a program that leaves them out, or rounds other values in their place, can miss the bound.
Values may be sent and summed in bfloat16 or wider, within the bound.
No kernel may reach another device: no remote copies, remote signals or barrier semaphores. Data moves between devices by JAX's collectives and lax.ppermute only.
A program may use at most 64 MiB of HBM per device.

v0:
```python
import math

import jax
import jax.numpy as jnp
from jax import lax
from jax.sharding import PartitionSpec as P

HD = 128
TXT = 512
GRID_W = 64
GROUP = 16


EPSILON = 1e-06
THETA = 10000.0


def in_one_piece(arrays, axis, split_dim, concat_dim, along):
    both = jnp.concatenate(arrays, axis=along)
    out, at, finished = (
        lax.all_to_all(both, axis, split_axis=split_dim, concat_axis=concat_dim, tiled=True),
        0,
        [],
    )
    for a in arrays:
        finished.append(lax.slice_in_dim(out, at, at + a.shape[along], axis=along))
        at += a.shape[along]
    return tuple(finished)


def passed_along(block, axis, distance):
    devices = range(lax.axis_size(axis))
    route = [((i - distance) % len(devices), i) for i in devices]
    return lax.ppermute(block, axis, route)


def rotation(first, count, head_dim):
    block_offsets = first + jnp.arange(count, dtype=jnp.int32)
    is_image = block_offsets >= TXT
    patch = jnp.maximum(block_offsets - TXT, 0)
    row_id = jnp.where(is_image, patch // GRID_W, 0).astype(jnp.float32)
    column_id = jnp.where(is_image, patch % GRID_W, 0).astype(jnp.float32)
    leading = head_dim // 8
    lateral = (head_dim - leading) // 2
    exponent = jnp.arange(lateral // 2, dtype=jnp.float32) * (2.0 / lateral)
    frequency = jnp.exp(-math.log(THETA) * exponent)
    angles = jnp.concatenate(
        [
            jnp.zeros((count, leading // 2), jnp.float32),
            row_id[:, None] * frequency[None, :],
            column_id[:, None] * frequency[None, :],
        ],
        axis=1,
    )
    angles = jnp.repeat(angles, 2, axis=1)
    return (jnp.cos(angles), jnp.sin(angles))


def rotation_partner(head_dim):
    across = jnp.arange(head_dim, dtype=jnp.int32)
    lower = across[:, None]
    upper = across[None, :]
    forward = ((upper == lower + 1) & (lower % 2 == 0)).astype(jnp.float32)
    backward = ((lower == upper + 1) & (upper % 2 == 0)).astype(jnp.float32)
    return forward - backward


def normalize(raw, tangent, gain, cosine, sine, partner):
    values = raw.astype(jnp.float32)
    motion = tangent.astype(jnp.float32)
    inverse = lax.rsqrt(jnp.mean(values * values, axis=-1, keepdims=True) + EPSILON)
    coupling = jnp.mean(values * motion, axis=-1, keepdims=True)
    normed = values * inverse * gain
    normalized_tangent = gain * (motion * inverse - values * inverse * inverse * inverse * coupling)

    def rotate(feature_field):
        return (
            feature_field * cosine
            + jnp.dot(feature_field, partner, precision=lax.Precision.HIGHEST) * sine
        )

    return (rotate(normed).astype(jnp.bfloat16), rotate(normalized_tangent).astype(jnp.bfloat16))


def local(
    query_rows,
    key_rows,
    value_rows,
    query_tangent,
    key_tangent,
    value_tangent,
    query_gain,
    key_gain,
):
    arrived = in_one_piece(
        (query_rows, key_rows, value_rows, query_tangent, key_tangent, value_tangent),
        "head",
        2,
        1,
        0,
    )
    rows_here = arrived[0].shape[1]
    local_width = arrived[0].shape[2]
    heads_here = local_width // HD
    images = lax.axis_size("blk") // GROUP
    place = lax.axis_index("blk") // images

    def split_heads(feature_field):
        return feature_field[0].reshape(rows_here, heads_here, HD)

    cosine, sine = rotation(place * rows_here, rows_here, HD)
    cosine = cosine[:, None, :]
    sine = sine[:, None, :]
    partner = rotation_partner(HD)
    query_hat, query_dot = normalize(
        split_heads(arrived[0]), split_heads(arrived[3]), query_gain, cosine, sine, partner
    )
    key_hat, key_dot = normalize(
        split_heads(arrived[1]), split_heads(arrived[4]), key_gain, cosine, sine, partner
    )
    own_block = jnp.stack(
        [
            key_hat.reshape(rows_here, local_width),
            arrived[2][0],
            key_dot.reshape(rows_here, local_width),
            arrived[5][0],
        ],
        axis=0,
    )
    scale = 1.0 / math.sqrt(HD)
    query_pair = jnp.concatenate([query_dot, query_hat], axis=2)

    def absorb_segment(state, key_block):
        peak, total, drift, summed, summed_dot = state
        count = key_block.shape[1]
        block_key = key_block[0].reshape(count, heads_here, HD)
        block_value = key_block[1].reshape(count, heads_here, HD)
        block_key_dot = key_block[2].reshape(count, heads_here, HD)
        block_value_dot = key_block[3].reshape(count, heads_here, HD)
        logit_scores = (
            jnp.einsum("qhd,khd->hqk", query_hat, block_key, preferred_element_type=jnp.float32)
            * scale
        )
        key_pair = jnp.concatenate([block_key, block_key_dot], axis=2)
        score_dot = (
            jnp.einsum("qhd,khd->hqk", query_pair, key_pair, preferred_element_type=jnp.float32)
            * scale
        )
        new_peak = jnp.maximum(peak, jnp.max(logit_scores, axis=2, keepdims=True))
        rescale = jnp.exp(peak - new_peak)
        weights = jnp.exp(logit_scores - new_peak)
        product = weights * score_dot
        total = total * rescale + jnp.sum(weights, axis=2, keepdims=True)
        drift = drift * rescale + jnp.sum(product, axis=2, keepdims=True)
        low_weights = weights.astype(jnp.bfloat16)
        low_product = product.astype(jnp.bfloat16)
        summed = summed * rescale + jnp.einsum(
            "hqk,khd->hqd", low_weights, block_value, preferred_element_type=jnp.float32
        )
        summed_dot = (
            summed_dot * rescale
            + jnp.einsum(
                "hqk,khd->hqd", low_weights, block_value_dot, preferred_element_type=jnp.float32
            )
            + jnp.einsum(
                "hqk,khd->hqd", low_product, block_value, preferred_element_type=jnp.float32
            )
        )
        return (new_peak, total, drift, summed, summed_dot)

    def absorb(state, key_block):
        count = key_block.shape[1]
        span = 2 * rows_here
        return absorb_segment(state, key_block)

    state = (
        jnp.full((heads_here, rows_here, 1), -jnp.inf, jnp.float32),
        jnp.zeros((heads_here, rows_here, 1), jnp.float32),
        jnp.zeros((heads_here, rows_here, 1), jnp.float32),
        jnp.zeros((heads_here, rows_here, HD), jnp.float32),
        jnp.zeros((heads_here, rows_here, HD), jnp.float32),
    )

    def step_up(key_block):
        return passed_along(key_block, "blk", images)

    def both_step(counter, carry):
        carried, upward, downward = carry
        upward = step_up(upward)
        downward = passed_along(downward, "blk", -images)
        carried = absorb(carried, jnp.concatenate([upward, downward], axis=1))
        return (carried, upward, downward)

    state, upward, downward = lax.fori_loop(
        0, GROUP // 2 - 1, both_step, (state, own_block, own_block)
    )
    farthest = step_up(upward)
    state = absorb(state, jnp.concatenate([own_block, farthest], axis=1))
    peak, total, drift, summed, summed_dot = state
    attention_output = summed / total
    output_tangent = (summed_dot - drift / total * summed) / total
    attention_output = (
        attention_output.transpose(1, 0, 2)
        .reshape(rows_here, local_width)
        .astype(jnp.bfloat16)[None]
    )
    output_tangent = (
        output_tangent.transpose(1, 0, 2).reshape(rows_here, local_width).astype(jnp.bfloat16)[None]
    )
    returned = in_one_piece((attention_output, output_tangent), "head", 1, 2, 0)
    return (returned[0], returned[1])


def solution(mesh):
    in_specs = (
        P("blk", "head", None),
        P("blk", "head", None),
        P("blk", "head", None),
        P("blk", "head", None),
        P("blk", "head", None),
        P("blk", "head", None),
        P(),
        P(),
    )
    out_specs = (P("blk", "head", None), P("blk", "head", None))
    return jax.shard_map(local, mesh=mesh, in_specs=in_specs, out_specs=out_specs, check_vma=False)
```

profile of v0, /device:TPU:6, one launch (start us, length us, event | category | flops | bytes accessed | tf_op | source)
XLA Modules:
  0.0 282.4 jit_solution(160029324533516999)
XLA Ops:
  6.2 5.8 %copy.134 = bf16[6,18,3072]{1,0,2:T(8,128)(2,1)} copy(bf16[6,18,3072]{2,1,0:T(8,128)(2,1)S(1)} %constant_dynamic-update-slice_fusion.2) | data formatting | bytes 1327104 | tf_op jit(solution)/shard_map/concatenate | solution.py:19
  12.0 9.6 %reshape.168 = bf16[8,2,20736]{2,1,0:T(2,128)(2,1)} reshape(bf16[3072,6,18]{2,1,0:T(8,128)(2,1)} %bitcast.97) | data formatting | bytes 1327104
  21.5 7.1 %all-to-all-start = ((bf16[8,2,20736]{2,1,0:T(2,128)(2,1)}), bf16[8,2,20736]{2,1,0:T(2,128)(2,1)S(1)}, u32[]{:S(2)}, u32[]{:S(2)}) async-start(bf16[8,2,20736]{2,1,0:T(2,128)(2,1)} %reshape.168), calls=%async_computation | async-start | bytes 1327104 | tf_op jit(solution)/shard_map/all_to_all | solution.py:21
  29.7 19.6 %all-to-all-done = bf16[8,2,20736]{2,1,0:T(2,128)(2,1)S(1)} async-done(((bf16[8,2,20736]{2,1,0:T(2,128)(2,1)}), bf16[8,2,20736]{2,1,0:T(2,128)(2,1)S(1)}, u32[]{:S(2)}, u32[]{:S(2)}) %all-to-all-start) | async-done | bytes 663584 | tf_op jit(solution)/shard_map/all_to_all | solution.py:21
  49.3 8.0 %reshape.169 = bf16[3072,6,18]{2,1,0:T(8,128)(2,1)} reshape(bf16[8,2,20736]{2,1,0:T(2,128)(2,1)S(1)} %all-to-all-done) | data formatting | bytes 1327104
  57.3 6.4 %copy.135 = bf16[6,18,8,384]{3,1,2,0:T(8,128)(2,1)S(1)} copy(bf16[6,18,8,384]{1,0,3,2:T(8,128)(2,1)} %bitcast.98) | data formatting | bytes 1327104 | tf_op jit(solution)/shard_map/all_to_all | solution.py:21
  68.6 169.1 %while.23 = (s32[]{:T(128)}, f32[3,144,1]{1,0,2:T(4,128)S(1)}, f32[3,144,1]{1,0,2:T(4,128)S(1)}, f32[3,144,1]{1,0,2:T(4,128)S(1)}, f32[3,144,128]{2,1,0:T(8,128)...) while((s32[]{:T(128)}, f32[3,144,1]{1,0,2:T(4,128)S(1)}, ...), condition=%wide.region_8.9_spmd.clone, body=%wide.region_4.8_spmd.clone.sunk | while | flops 193995648 | bytes 17513496 | solution.py:194
  70.5 9.1 %collective-permute-start.1 = (bf16[4,144,384]{2,1,0:T(8,128)(2,1)S(1)}, bf16[4,144,384]{2,1,0:T(8,128)(2,1)S(1)}, u32[]{:S(2)}, u32[]{:S(2)}) collective-permute-start(bf16[4,144,384]{2,1,0:T(8,128)(2,1)S(1)} %get-tuple-element.271), channel_id=1, source_target_pairs={{4,0},{5,1},{6,2},{7,3},{8,4},{9,5},{10,6},{11,7},{12,8},{13,9},{1... | collective-permute-start | bytes 1327112 | tf_op jit(solution)/shard_map/while/body/eval_jaxpr/ppermute | solution.py:34
  79.7 9.1 %collective-permute-done = bf16[4,144,384]{2,1,0:T(8,128)(2,1)S(1)} collective-permute-done((bf16[4,144,384]{2,1,0:T(8,128)(2,1)S(1)}, bf16[4,144,384]{2,1,0:T(8,128)(2,1)S(1)}, u32[]{:S(2)}, u32[]{:S(2)}) %collective-permute-start) | collective-permute-done | bytes 442400 | tf_op jit(solution)/shard_map/while/body/eval_jaxpr/ppermute | solution.py:34
  98.0 6.4 %collective-permute-start.1 = (bf16[4,144,384]{2,1,0:T(8,128)(2,1)S(1)}, bf16[4,144,384]{2,1,0:T(8,128)(2,1)S(1)}, u32[]{:S(2)}, u32[]{:S(2)}) collective-permute-start(bf16[4,144,384]{2,1,0:T(8,128)(2,1)S(1)} %get-tuple-element.271), channel_id=1, source_target_pairs={{4,0},{5,1},{6,2},{7,3},{8,4},{9,5},{10,6},{11,7},{12,8},{13,9},{1... | collective-permute-start | bytes 1327112 | tf_op jit(solution)/shard_map/while/body/eval_jaxpr/ppermute | solution.py:34
  104.4 9.1 %collective-permute-done = bf16[4,144,384]{2,1,0:T(8,128)(2,1)S(1)} collective-permute-done((bf16[4,144,384]{2,1,0:T(8,128)(2,1)S(1)}, bf16[4,144,384]{2,1,0:T(8,128)(2,1)S(1)}, u32[]{:S(2)}, u32[]{:S(2)}) %collective-permute-start) | collective-permute-done | bytes 442400 | tf_op jit(solution)/shard_map/while/body/eval_jaxpr/ppermute | solution.py:34
  113.5 4.4 %collective-permute-done.1 = bf16[4,144,384]{2,1,0:T(8,128)(2,1)S(1)} collective-permute-done((bf16[4,144,384]{2,1,0:T(8,128)(2,1)S(1)}, bf16[4,144,384]{2,1,0:T(8,128)(2,1)S(1)}, u32[]{:S(2)}, u32[]{:S(2)}) %collective-permute-start.1) | collective-permute-done | bytes 442400 | tf_op jit(solution)/shard_map/while/body/eval_jaxpr/ppermute | solution.py:34
  124.5 5.1 %collective-permute-start.1 = (bf16[4,144,384]{2,1,0:T(8,128)(2,1)S(1)}, bf16[4,144,384]{2,1,0:T(8,128)(2,1)S(1)}, u32[]{:S(2)}, u32[]{:S(2)}) collective-permute-start(bf16[4,144,384]{2,1,0:T(8,128)(2,1)S(1)} %get-tuple-element.271), channel_id=1, source_target_pairs={{4,0},{5,1},{6,2},{7,3},{8,4},{9,5},{10,6},{11,7},{12,8},{13,9},{1... | collective-permute-start | bytes 1327112 | tf_op jit(solution)/shard_map/while/body/eval_jaxpr/ppermute | solution.py:34
  129.6 9.1 %collective-permute-done = bf16[4,144,384]{2,1,0:T(8,128)(2,1)S(1)} collective-permute-done((bf16[4,144,384]{2,1,0:T(8,128)(2,1)S(1)}, bf16[4,144,384]{2,1,0:T(8,128)(2,1)S(1)}, u32[]{:S(2)}, u32[]{:S(2)}) %collective-permute-start) | collective-permute-done | bytes 442400 | tf_op jit(solution)/shard_map/while/body/eval_jaxpr/ppermute | solution.py:34
  138.7 4.4 %collective-permute-done.1 = bf16[4,144,384]{2,1,0:T(8,128)(2,1)S(1)} collective-permute-done((bf16[4,144,384]{2,1,0:T(8,128)(2,1)S(1)}, bf16[4,144,384]{2,1,0:T(8,128)(2,1)S(1)}, u32[]{:S(2)}, u32[]{:S(2)}) %collective-permute-start.1) | collective-permute-done | bytes 442400 | tf_op jit(solution)/shard_map/while/body/eval_jaxpr/ppermute | solution.py:34
  150.3 4.6 %collective-permute-start.1 = (bf16[4,144,384]{2,1,0:T(8,128)(2,1)S(1)}, bf16[4,144,384]{2,1,0:T(8,128)(2,1)S(1)}, u32[]{:S(2)}, u32[]{:S(2)}) collective-permute-start(bf16[4,144,384]{2,1,0:T(8,128)(2,1)S(1)} %get-tuple-element.271), channel_id=1, source_target_pairs={{4,0},{5,1},{6,2},{7,3},{8,4},{9,5},{10,6},{11,7},{12,8},{13,9},{1... | collective-permute-start | bytes 1327112 | tf_op jit(solution)/shard_map/while/body/eval_jaxpr/ppermute | solution.py:34
  154.8 8.2 %collective-permute-done = bf16[4,144,384]{2,1,0:T(8,128)(2,1)S(1)} collective-permute-done((bf16[4,144,384]{2,1,0:T(8,128)(2,1)S(1)}, bf16[4,144,384]{2,1,0:T(8,128)(2,1)S(1)}, u32[]{:S(2)}, u32[]{:S(2)}) %collective-permute-start) | collective-permute-done | bytes 442400 | tf_op jit(solution)/shard_map/while/body/eval_jaxpr/ppermute | solution.py:34
  163.1 5.3 %collective-permute-done.1 = bf16[4,144,384]{2,1,0:T(8,128)(2,1)S(1)} collective-permute-done((bf16[4,144,384]{2,1,0:T(8,128)(2,1)S(1)}, bf16[4,144,384]{2,1,0:T(8,128)(2,1)S(1)}, u32[]{:S(2)}, u32[]{:S(2)}) %collective-permute-start.1) | collective-permute-done | bytes 442400 | tf_op jit(solution)/shard_map/while/body/eval_jaxpr/ppermute | solution.py:34
  172.1 4.2 %collective-permute-start = (bf16[4,144,384]{2,1,0:T(8,128)(2,1)S(1)}, bf16[4,144,384]{2,1,0:T(8,128)(2,1)S(1)}, u32[]{:S(2)}, u32[]{:S(2)}) collective-permute-start(bf16[4,144,384]{2,1,0:T(8,128)(2,1)S(1)} %get-tuple-element.270), channel_id=1, source_target_pairs={{60,0},{61,1},{62,2},{63,3},{0,4},{1,5},{2,6},{3,7},{4,8},{5,9},{6... | collective-permute-start | bytes 1327112 | tf_op jit(solution)/shard_map/while/body/eval_jaxpr/ppermute | solution.py:34
  176.3 3.8 %collective-permute-start.1 = (bf16[4,144,384]{2,1,0:T(8,128)(2,1)S(1)}, bf16[4,144,384]{2,1,0:T(8,128)(2,1)S(1)}, u32[]{:S(2)}, u32[]{:S(2)}) collective-permute-start(bf16[4,144,384]{2,1,0:T(8,128)(2,1)S(1)} %get-tuple-element.271), channel_id=1, source_target_pairs={{4,0},{5,1},{6,2},{7,3},{8,4},{9,5},{10,6},{11,7},{12,8},{13,9},{1... | collective-permute-start | bytes 1327112 | tf_op jit(solution)/shard_map/while/body/eval_jaxpr/ppermute | solution.py:34
  180.1 7.0 %collective-permute-done = bf16[4,144,384]{2,1,0:T(8,128)(2,1)S(1)} collective-permute-done((bf16[4,144,384]{2,1,0:T(8,128)(2,1)S(1)}, bf16[4,144,384]{2,1,0:T(8,128)(2,1)S(1)}, u32[]{:S(2)}, u32[]{:S(2)}) %collective-permute-start) | collective-permute-done | bytes 442400 | tf_op jit(solution)/shard_map/while/body/eval_jaxpr/ppermute | solution.py:34
  187.1 4.1 %collective-permute-done.1 = bf16[4,144,384]{2,1,0:T(8,128)(2,1)S(1)} collective-permute-done((bf16[4,144,384]{2,1,0:T(8,128)(2,1)S(1)}, bf16[4,144,384]{2,1,0:T(8,128)(2,1)S(1)}, u32[]{:S(2)}, u32[]{:S(2)}) %collective-permute-start.1) | collective-permute-done | bytes 442400 | tf_op jit(solution)/shard_map/while/body/eval_jaxpr/ppermute | solution.py:34
  195.0 4.1 %collective-permute-start = (bf16[4,144,384]{2,1,0:T(8,128)(2,1)S(1)}, bf16[4,144,384]{2,1,0:T(8,128)(2,1)S(1)}, u32[]{:S(2)}, u32[]{:S(2)}) collective-permute-start(bf16[4,144,384]{2,1,0:T(8,128)(2,1)S(1)} %get-tuple-element.270), channel_id=1, source_target_pairs={{60,0},{61,1},{62,2},{63,3},{0,4},{1,5},{2,6},{3,7},{4,8},{5,9},{6... | collective-permute-start | bytes 1327112 | tf_op jit(solution)/shard_map/while/body/eval_jaxpr/ppermute | solution.py:34
  199.1 3.8 %collective-permute-start.1 = (bf16[4,144,384]{2,1,0:T(8,128)(2,1)S(1)}, bf16[4,144,384]{2,1,0:T(8,128)(2,1)S(1)}, u32[]{:S(2)}, u32[]{:S(2)}) collective-permute-start(bf16[4,144,384]{2,1,0:T(8,128)(2,1)S(1)} %get-tuple-element.271), channel_id=1, source_target_pairs={{4,0},{5,1},{6,2},{7,3},{8,4},{9,5},{10,6},{11,7},{12,8},{13,9},{1... | collective-permute-start | bytes 1327112 | tf_op jit(solution)/shard_map/while/body/eval_jaxpr/ppermute | solution.py:34
  202.9 6.5 %collective-permute-done = bf16[4,144,384]{2,1,0:T(8,128)(2,1)S(1)} collective-permute-done((bf16[4,144,384]{2,1,0:T(8,128)(2,1)S(1)}, bf16[4,144,384]{2,1,0:T(8,128)(2,1)S(1)}, u32[]{:S(2)}, u32[]{:S(2)}) %collective-permute-start) | collective-permute-done | bytes 442400 | tf_op jit(solution)/shard_map/while/body/eval_jaxpr/ppermute | solution.py:34
  209.4 3.5 %collective-permute-done.1 = bf16[4,144,384]{2,1,0:T(8,128)(2,1)S(1)} collective-permute-done((bf16[4,144,384]{2,1,0:T(8,128)(2,1)S(1)}, bf16[4,144,384]{2,1,0:T(8,128)(2,1)S(1)}, u32[]{:S(2)}, u32[]{:S(2)}) %collective-permute-start.1) | collective-permute-done | bytes 442400 | tf_op jit(solution)/shard_map/while/body/eval_jaxpr/ppermute | solution.py:34
  216.7 3.9 %collective-permute-start = (bf16[4,144,384]{2,1,0:T(8,128)(2,1)S(1)}, bf16[4,144,384]{2,1,0:T(8,128)(2,1)S(1)}, u32[]{:S(2)}, u32[]{:S(2)}) collective-permute-start(bf16[4,144,384]{2,1,0:T(8,128)(2,1)S(1)} %get-tuple-element.270), channel_id=1, source_target_pairs={{60,0},{61,1},{62,2},{63,3},{0,4},{1,5},{2,6},{3,7},{4,8},{5,9},{6... | collective-permute-start | bytes 1327112 | tf_op jit(solution)/shard_map/while/body/eval_jaxpr/ppermute | solution.py:34
  220.7 4.0 %collective-permute-start.1 = (bf16[4,144,384]{2,1,0:T(8,128)(2,1)S(1)}, bf16[4,144,384]{2,1,0:T(8,128)(2,1)S(1)}, u32[]{:S(2)}, u32[]{:S(2)}) collective-permute-start(bf16[4,144,384]{2,1,0:T(8,128)(2,1)S(1)} %get-tuple-element.271), channel_id=1, source_target_pairs={{4,0},{5,1},{6,2},{7,3},{8,4},{9,5},{10,6},{11,7},{12,8},{13,9},{1... | collective-permute-start | bytes 1327112 | tf_op jit(solution)/shard_map/while/body/eval_jaxpr/ppermute | solution.py:34
  224.7 5.6 %collective-permute-done = bf16[4,144,384]{2,1,0:T(8,128)(2,1)S(1)} collective-permute-done((bf16[4,144,384]{2,1,0:T(8,128)(2,1)S(1)}, bf16[4,144,384]{2,1,0:T(8,128)(2,1)S(1)}, u32[]{:S(2)}, u32[]{:S(2)}) %collective-permute-start) | collective-permute-done | bytes 442400 | tf_op jit(solution)/shard_map/while/body/eval_jaxpr/ppermute | solution.py:34
  230.3 3.6 %collective-permute-done.1 = bf16[4,144,384]{2,1,0:T(8,128)(2,1)S(1)} collective-permute-done((bf16[4,144,384]{2,1,0:T(8,128)(2,1)S(1)}, bf16[4,144,384]{2,1,0:T(8,128)(2,1)S(1)}, u32[]{:S(2)}, u32[]{:S(2)}) %collective-permute-start.1) | collective-permute-done | bytes 442400 | tf_op jit(solution)/shard_map/while/body/eval_jaxpr/ppermute | solution.py:34
  241.2 8.8 %collective-permute-done.2 = bf16[4,144,384]{2,1,0:T(8,128)(2,1)S(1)} collective-permute-done((bf16[4,144,384]{2,1,0:T(8,128)(2,1)S(1)}, bf16[4,144,384]{2,1,0:T(8,128)(2,1)S(1)}, u32[]{:S(2)}, u32[]{:S(2)}) %collective-permute-start.2) | collective-permute-done | bytes 442400 | tf_op jit(solution)/shard_map/ppermute | solution.py:34
  255.3 25.3 %all_to_all.30 = bf16[2,144,384]{2,0,1:T(2,128)(2,1)S(1)} all-to-all(bf16[2,144,384]{2,0,1:T(2,128)(2,1)S(1)} %copy.156), channel_id=1, replica_groups=mesh['head'=8,'blk'=64] {'head'}, dimensions={1} | all-to-all | bytes 442368 | tf_op jit(solution)/shard_map/all_to_all | solution.py:21
  (236 shorter events, 61.0 us)
Async XLA Ops:
  21.5 27.8 %all-to-all-start = ((bf16[8,2,20736]{2,1,0:T(2,128)(2,1)}), bf16[8,2,20736]{2,1,0:T(2,128)(2,1)S(1)}, u32[]{:S(2)}, u32[]{:S(2)}) async-start(bf16[8,2,20736]{2,1,0:T(2,128)(2,1)} %reshape.168), calls=%async_computation | async-start | bytes 1327104 | tf_op jit(solution)/shard_map/all_to_all | solution.py:21
  57.3 7.3 %copy-start.2 = (f32[128]{0:T(128)S(1)}, f32[128]{0:T(128)}, u32[]{:S(2)}) copy-start(f32[128]{0:T(128)} %param.17) | copy-start | bytes 1540
  63.7 3.2 %copy-start.3 = (f32[128]{0:T(128)S(1)}, f32[128]{0:T(128)}, u32[]{:S(2)}) copy-start(f32[128]{0:T(128)} %param.16) | copy-start | bytes 1540
  66.1 0.9 copy-start
  67.9 0.7 copy-start.1
  68.6 20.1 %collective-permute-start = (bf16[4,144,384]{2,1,0:T(8,128)(2,1)S(1)}, bf16[4,144,384]{2,1,0:T(8,128)(2,1)S(1)}, u32[]{:S(2)}, u32[]{:S(2)}) collective-permute-start(bf16[4,144,384]{2,1,0:T(8,128)(2,1)S(1)} %get-tuple-element.270), channel_id=1, source_target_pairs={{60,0},{61,1},{62,2},{63,3},{0,4},{1,5},{2,6},{3,7},{4,8},{5,9},{6... | collective-permute-start | bytes 1327112 | tf_op jit(solution)/shard_map/while/body/eval_jaxpr/ppermute | solution.py:34
  70.5 21.2 %collective-permute-start.1 = (bf16[4,144,384]{2,1,0:T(8,128)(2,1)S(1)}, bf16[4,144,384]{2,1,0:T(8,128)(2,1)S(1)}, u32[]{:S(2)}, u32[]{:S(2)}) collective-permute-start(bf16[4,144,384]{2,1,0:T(8,128)(2,1)S(1)} %get-tuple-element.271), channel_id=1, source_target_pairs={{4,0},{5,1},{6,2},{7,3},{8,4},{9,5},{10,6},{11,7},{12,8},{13,9},{1... | collective-permute-start | bytes 1327112 | tf_op jit(solution)/shard_map/while/body/eval_jaxpr/ppermute | solution.py:34
  95.5 17.9 %collective-permute-start = (bf16[4,144,384]{2,1,0:T(8,128)(2,1)S(1)}, bf16[4,144,384]{2,1,0:T(8,128)(2,1)S(1)}, u32[]{:S(2)}, u32[]{:S(2)}) collective-permute-start(bf16[4,144,384]{2,1,0:T(8,128)(2,1)S(1)} %get-tuple-element.270), channel_id=1, source_target_pairs={{60,0},{61,1},{62,2},{63,3},{0,4},{1,5},{2,6},{3,7},{4,8},{5,9},{6... | collective-permute-start | bytes 1327112 | tf_op jit(solution)/shard_map/while/body/eval_jaxpr/ppermute | solution.py:34
  98.0 19.9 %collective-permute-start.1 = (bf16[4,144,384]{2,1,0:T(8,128)(2,1)S(1)}, bf16[4,144,384]{2,1,0:T(8,128)(2,1)S(1)}, u32[]{:S(2)}, u32[]{:S(2)}) collective-permute-start(bf16[4,144,384]{2,1,0:T(8,128)(2,1)S(1)} %get-tuple-element.271), channel_id=1, source_target_pairs={{4,0},{5,1},{6,2},{7,3},{8,4},{9,5},{10,6},{11,7},{12,8},{13,9},{1... | collective-permute-start | bytes 1327112 | tf_op jit(solution)/shard_map/while/body/eval_jaxpr/ppermute | solution.py:34
  121.6 17.0 %collective-permute-start = (bf16[4,144,384]{2,1,0:T(8,128)(2,1)S(1)}, bf16[4,144,384]{2,1,0:T(8,128)(2,1)S(1)}, u32[]{:S(2)}, u32[]{:S(2)}) collective-permute-start(bf16[4,144,384]{2,1,0:T(8,128)(2,1)S(1)} %get-tuple-element.270), channel_id=1, source_target_pairs={{60,0},{61,1},{62,2},{63,3},{0,4},{1,5},{2,6},{3,7},{4,8},{5,9},{6... | collective-permute-start | bytes 1327112 | tf_op jit(solution)/shard_map/while/body/eval_jaxpr/ppermute | solution.py:34
  124.5 18.6 %collective-permute-start.1 = (bf16[4,144,384]{2,1,0:T(8,128)(2,1)S(1)}, bf16[4,144,384]{2,1,0:T(8,128)(2,1)S(1)}, u32[]{:S(2)}, u32[]{:S(2)}) collective-permute-start(bf16[4,144,384]{2,1,0:T(8,128)(2,1)S(1)} %get-tuple-element.271), channel_id=1, source_target_pairs={{4,0},{5,1},{6,2},{7,3},{8,4},{9,5},{10,6},{11,7},{12,8},{13,9},{1... | collective-permute-start | bytes 1327112 | tf_op jit(solution)/shard_map/while/body/eval_jaxpr/ppermute | solution.py:34
  146.9 16.2 %collective-permute-start = (bf16[4,144,384]{2,1,0:T(8,128)(2,1)S(1)}, bf16[4,144,384]{2,1,0:T(8,128)(2,1)S(1)}, u32[]{:S(2)}, u32[]{:S(2)}) collective-permute-start(bf16[4,144,384]{2,1,0:T(8,128)(2,1)S(1)} %get-tuple-element.270), channel_id=1, source_target_pairs={{60,0},{61,1},{62,2},{63,3},{0,4},{1,5},{2,6},{3,7},{4,8},{5,9},{6... | collective-permute-start | bytes 1327112 | tf_op jit(solution)/shard_map/while/body/eval_jaxpr/ppermute | solution.py:34
  150.3 18.1 %collective-permute-start.1 = (bf16[4,144,384]{2,1,0:T(8,128)(2,1)S(1)}, bf16[4,144,384]{2,1,0:T(8,128)(2,1)S(1)}, u32[]{:S(2)}, u32[]{:S(2)}) collective-permute-start(bf16[4,144,384]{2,1,0:T(8,128)(2,1)S(1)} %get-tuple-element.271), channel_id=1, source_target_pairs={{4,0},{5,1},{6,2},{7,3},{8,4},{9,5},{10,6},{11,7},{12,8},{13,9},{1... | collective-permute-start | bytes 1327112 | tf_op jit(solution)/shard_map/while/body/eval_jaxpr/ppermute | solution.py:34
  172.1 15.0 %collective-permute-start = (bf16[4,144,384]{2,1,0:T(8,128)(2,1)S(1)}, bf16[4,144,384]{2,1,0:T(8,128)(2,1)S(1)}, u32[]{:S(2)}, u32[]{:S(2)}) collective-permute-start(bf16[4,144,384]{2,1,0:T(8,128)(2,1)S(1)} %get-tuple-element.270), channel_id=1, source_target_pairs={{60,0},{61,1},{62,2},{63,3},{0,4},{1,5},{2,6},{3,7},{4,8},{5,9},{6... | collective-permute-start | bytes 1327112 | tf_op jit(solution)/shard_map/while/body/eval_jaxpr/ppermute | solution.py:34
  176.3 14.9 %collective-permute-start.1 = (bf16[4,144,384]{2,1,0:T(8,128)(2,1)S(1)}, bf16[4,144,384]{2,1,0:T(8,128)(2,1)S(1)}, u32[]{:S(2)}, u32[]{:S(2)}) collective-permute-start(bf16[4,144,384]{2,1,0:T(8,128)(2,1)S(1)} %get-tuple-element.271), channel_id=1, source_target_pairs={{4,0},{5,1},{6,2},{7,3},{8,4},{9,5},{10,6},{11,7},{12,8},{13,9},{1... | collective-permute-start | bytes 1327112 | tf_op jit(solution)/shard_map/while/body/eval_jaxpr/ppermute | solution.py:34
  195.0 14.4 %collective-permute-start = (bf16[4,144,384]{2,1,0:T(8,128)(2,1)S(1)}, bf16[4,144,384]{2,1,0:T(8,128)(2,1)S(1)}, u32[]{:S(2)}, u32[]{:S(2)}) collective-permute-start(bf16[4,144,384]{2,1,0:T(8,128)(2,1)S(1)} %get-tuple-element.270), channel_id=1, source_target_pairs={{60,0},{61,1},{62,2},{63,3},{0,4},{1,5},{2,6},{3,7},{4,8},{5,9},{6... | collective-permute-start | bytes 1327112 | tf_op jit(solution)/shard_map/while/body/eval_jaxpr/ppermute | solution.py:34
  199.1 13.9 %collective-permute-start.1 = (bf16[4,144,384]{2,1,0:T(8,128)(2,1)S(1)}, bf16[4,144,384]{2,1,0:T(8,128)(2,1)S(1)}, u32[]{:S(2)}, u32[]{:S(2)}) collective-permute-start(bf16[4,144,384]{2,1,0:T(8,128)(2,1)S(1)} %get-tuple-element.271), channel_id=1, source_target_pairs={{4,0},{5,1},{6,2},{7,3},{8,4},{9,5},{10,6},{11,7},{12,8},{13,9},{1... | collective-permute-start | bytes 1327112 | tf_op jit(solution)/shard_map/while/body/eval_jaxpr/ppermute | solution.py:34
  216.7 13.6 %collective-permute-start = (bf16[4,144,384]{2,1,0:T(8,128)(2,1)S(1)}, bf16[4,144,384]{2,1,0:T(8,128)(2,1)S(1)}, u32[]{:S(2)}, u32[]{:S(2)}) collective-permute-start(bf16[4,144,384]{2,1,0:T(8,128)(2,1)S(1)} %get-tuple-element.270), channel_id=1, source_target_pairs={{60,0},{61,1},{62,2},{63,3},{0,4},{1,5},{2,6},{3,7},{4,8},{5,9},{6... | collective-permute-start | bytes 1327112 | tf_op jit(solution)/shard_map/while/body/eval_jaxpr/ppermute | solution.py:34
  220.7 13.3 %collective-permute-start.1 = (bf16[4,144,384]{2,1,0:T(8,128)(2,1)S(1)}, bf16[4,144,384]{2,1,0:T(8,128)(2,1)S(1)}, u32[]{:S(2)}, u32[]{:S(2)}) collective-permute-start(bf16[4,144,384]{2,1,0:T(8,128)(2,1)S(1)} %get-tuple-element.271), channel_id=1, source_target_pairs={{4,0},{5,1},{6,2},{7,3},{8,4},{9,5},{10,6},{11,7},{12,8},{13,9},{1... | collective-permute-start | bytes 1327112 | tf_op jit(solution)/shard_map/while/body/eval_jaxpr/ppermute | solution.py:34
  237.7 12.3 %collective-permute-start.2 = (bf16[4,144,384]{2,1,0:T(8,128)(2,1)S(1)}, bf16[4,144,384]{2,1,0:T(8,128)(2,1)S(1)}, u32[]{:S(2)}, u32[]{:S(2)}) collective-permute-start(bf16[4,144,384]{2,1,0:T(8,128)(2,1)S(1)} %get-tuple-element.61), channel_id=1, source_target_pairs={{60,0},{61,1},{62,2},{63,3},{0,4},{1,5},{2,6},{3,7},{4,8},{5,9},{6... | collective-permute-start | bytes 1327112 | tf_op jit(solution)/shard_map/ppermute | solution.py:34
where the time goes:
time: 285 us; the launch traced here: 282 us
  waiting for transfers between devices  111 us (39%)
  starting transfers between devices  70.2 us (25%)
  local copies, waits for them, and re-layouts  44.1 us (15%)
  blocking collectives  25.3 us (9%)
  matrix products  23.3 us (8%)
  other arithmetic  6.41 us (2%)
    ppermute x15, waiting for transfers between devices, passed_along(): return lax.ppermute(block, axis, route)  91.5 us
    ppermute x15, starting transfers between devices, passed_along(): return lax.ppermute(block, axis, route)  63 us
    all_to_all x1, blocking collectives, in_one_piece(): lax.all_to_all(both, axis, split_axis=split_dim, concat_axis=concat_dim,...  25.3 us
    unnamed x20, local copies, waits for them, and re-layouts  22.4 us
    all_to_all x1, waiting for transfers between devices, in_one_piece(): lax.all_to_all(both, axis, split_axis=split_dim, concat_axis=concat_dim,...  19.6 us
    dot_general x8, matrix products, absorb_segment(): jnp.einsum('qhd,khd->hqk', query_pair, key_pair, preferred_element_type=j...  11 us
    all_to_all x1, starting transfers between devices, in_one_piece(): lax.all_to_all(both, axis, split_axis=split_dim, concat_axis=concat_dim,...  7.1 us
    concatenate x3, local copies, waits for them, and re-layouts, in_one_piece(): both = jnp.concatenate(arrays, axis=along)  6.88 us
  transfers between devices with their start and end apart: 16, of which 16 were waited for; matrix products, arithmetic and copies ran while one was open for 0% of the time, Pallas kernels for 0%

commit v1 on v0

v1 whole, which is shorter than its diff:
```python
import math

import jax
import jax.numpy as jnp
from jax import lax
from jax.experimental import pallas as pl
from jax.experimental.pallas import tpu as pltpu
from jax.sharding import Mesh
from jax.sharding import PartitionSpec as P

HEADS = 24
HD = 128
D = 3072
TXT = 512
GRID_W = 64
ROWS = 144
LOCAL = 18
MAIN = 16
SLOTS = 32
SRC_ROWS = 576
SEND = 112
BACK = 40
EPSILON = 1e-06
THETA = 10000.0
SCALE = 1.0 / math.sqrt(HD)
F32 = jnp.float32
BF16 = jnp.bfloat16

VMEM = pl.BlockSpec(memory_space=pltpu.VMEM)
SMEM = pl.BlockSpec(memory_space=pltpu.SMEM)


def slot_of(head):
    return (head % 3) * 8 + head // 3


def lanes(head):
    return slice(head * HD, (head + 1) * HD)


def one_hot(shape, column_of_row, valid):
    row = lax.broadcasted_iota(jnp.int32, shape, 0)
    column = lax.broadcasted_iota(jnp.int32, shape, 1)
    return jnp.where((column == column_of_row(row)) & valid(row), 1.0, 0.0).astype(BF16)


def prepare(first, query, key, value, query_t, key_t, value_t, query_gain, key_gain, out, tails):
    token = first[0] + lax.broadcasted_iota(jnp.int32, (LOCAL, HD), 0)
    lane = lax.broadcasted_iota(jnp.int32, (LOCAL, HD), 1)
    patch = jnp.maximum(token - TXT, 0)
    is_image = token >= TXT
    row_id = jnp.where(is_image, lax.shift_right_logical(patch, 6), 0).astype(F32)
    column_id = jnp.where(is_image, patch & (GRID_W - 1), 0).astype(F32)
    pair = lax.shift_right_logical(lane, 1)
    of_row = pair < 36
    step = jnp.where(of_row, pair - 8, pair - 36).astype(F32)
    frequency = jnp.exp(-math.log(THETA) * (step * (2.0 / 56.0)))
    angle = jnp.where(pair < 8, 0.0, jnp.where(of_row, row_id, column_id) * frequency)
    cosine = jnp.cos(angle)
    sine = jnp.sin(angle)
    even = (lane & 1) == 0
    sine_even = jnp.where(even, -sine, 0.0)
    sine_odd = jnp.where(even, 0.0, sine)

    def rotate(x):
        after = pltpu.roll(x, HD - 1, 1)
        before = pltpu.roll(x, 1, 1)
        return (x * cosine + after * sine_even + before * sine_odd).astype(BF16)

    def normalize(raw, tangent, gain):
        x = raw.astype(F32)
        u = tangent.astype(F32)
        inverse = lax.rsqrt(jnp.mean(x * x, axis=1, keepdims=True) + EPSILON)
        coupling = jnp.mean(x * u, axis=1, keepdims=True)
        xr = x * inverse
        normed = xr * gain
        dotted = gain * (u * inverse - xr * (inverse * inverse * coupling))
        return rotate(normed), rotate(dotted)

    tails[...] = jnp.zeros_like(tails)
    qg = query_gain[...]
    kg = key_gain[...]
    for head in range(HEADS):
        here = lanes(head)
        slot = slot_of(head)
        q_hat, q_dot = normalize(query[:, here], query_t[:, here], qg)
        k_hat, k_dot = normalize(key[:, here], key_t[:, here], kg)
        parts = (q_hat, q_dot, k_hat, k_dot, value[:, here], value_t[:, here])
        for t, part in enumerate(parts):
            out[slot, 16 * t : 16 * t + 16, :] = part[:MAIN]
            tails[16 * t : 16 * t + 2, here] = part[MAIN:]
    pick = one_hot((16, 96), lambda r: (r >> 1) * 16 + (r & 1), lambda r: r < 12)
    slab = jnp.dot(pick, tails[...], preferred_element_type=F32).astype(BF16)
    for head in range(HEADS):
        out[slot_of(head), 96:112, :] = slab[:, lanes(head)]
    for slot in range(HEADS, SLOTS):
        out[slot] = jnp.zeros((SEND, HD), BF16)


def repack(received, query_pair, key_value):
    places = ((query_pair, 128), (query_pair, 0)) + tuple((key_value, 128 * j) for j in range(4))
    for source in range(SLOTS):
        for t, (ref, at) in enumerate(places):
            ref[16 * source : 16 * source + 16, at : at + HD] = received[source, 16 * t : 16 * t + 16, :]
    slabs = received[:, 96:112, :].reshape(SLOTS * 16, HD)
    for t, (ref, at) in enumerate(places):
        pick = one_hot((64, 512), lambda r: (r >> 1) * 16 + 2 * t + (r & 1), lambda r: r >= 0)
        rest = jnp.dot(pick, slabs, preferred_element_type=F32).astype(BF16)
        ref[512:576, at : at + HD] = rest


TRANSPOSED = (((1,), (1,)), ((), ()))
BQ = 192


def attend(query_pair, kv0, kv1, kv2, kv3, out, attended, attended_t):
    blocks = (kv0, kv1, kv2, kv3)
    for b in range(SRC_ROWS // BQ):
        at = slice(b * BQ, (b + 1) * BQ)
        pair = query_pair[at, :]
        hat = query_pair[at, HD:]
        scores = [
            lax.dot_general(hat, kv[:, 0:HD], TRANSPOSED, preferred_element_type=F32) for kv in blocks
        ]
        peak = jnp.max(scores[0], axis=1, keepdims=True)
        for s in scores[1:]:
            peak = jnp.maximum(peak, jnp.max(s, axis=1, keepdims=True))
        total = drift = both = extra = 0.0
        for s, kv in zip(scores, blocks):
            weights = jnp.exp2((s - peak) * (SCALE * math.log2(math.e)))
            moved = lax.dot_general(pair, kv[:, 0 : 2 * HD], TRANSPOSED, preferred_element_type=F32)
            product = weights * (moved * SCALE)
            total = total + jnp.sum(weights, axis=1, keepdims=True)
            drift = drift + jnp.sum(product, axis=1, keepdims=True)
            both = both + jnp.dot(
                weights.astype(BF16), kv[:, 2 * HD : 4 * HD], preferred_element_type=F32
            )
            extra = extra + jnp.dot(
                product.astype(BF16), kv[:, 2 * HD : 3 * HD], preferred_element_type=F32
            )
        summed = both[:, :HD]
        summed_dot = both[:, HD:] + extra
        attended[at, :] = (summed / total).astype(BF16)
        attended_t[at, :] = ((summed_dot - drift / total * summed) / total).astype(BF16)
    for source in range(SLOTS):
        at = slice(16 * source, 16 * source + 16)
        out[source, 0:16, :] = attended[at, :]
        out[source, 16:32, :] = attended_t[at, :]
    rest = jnp.concatenate([attended[512:576, :], attended_t[512:576, :]], axis=0)
    pick = one_hot(
        (256, 128),
        lambda r: (r >> 3) * 2 + (r & 1) + jnp.where((r & 2) > 0, 64, 0),
        lambda r: (r & 7) < 4,
    )
    slabs = jnp.dot(pick, rest, preferred_element_type=F32).astype(BF16)
    out[:, 32:40, :] = slabs.reshape(SLOTS, 8, HD)


def unpack(received, attended, attended_t, tails):
    tails[...] = jnp.zeros_like(tails)
    for head in range(HEADS):
        slot = slot_of(head)
        here = lanes(head)
        attended[0:16, here] = received[slot, 0:16, :]
        attended_t[0:16, here] = received[slot, 16:32, :]
        tails[0:8, here] = received[slot, 32:40, :]
    pick = one_hot((16, 16), lambda r: jnp.where(r < 8, r, r - 6), lambda r: (r & 7) < 2)
    rest = jnp.dot(pick, tails[...], preferred_element_type=F32)
    attended[16:18, :] = rest[0:2].astype(BF16)
    attended_t[16:18, :] = rest[8:10].astype(BF16)


def local(query, key, value, query_t, key_t, value_t, query_gain, key_gain):
    place = lax.axis_index("z") * 2 + lax.axis_index("ylo")
    share = lax.axis_index("yhi") * 2 + lax.axis_index("core")
    first = (place * ROWS + share * LOCAL).reshape(1)
    rows = [a.reshape(LOCAL, D) for a in (query, key, value, query_t, key_t, value_t)]
    message = pl.pallas_call(
        prepare,
        out_shape=jax.ShapeDtypeStruct((SLOTS, SEND, HD), BF16),
        in_specs=[SMEM] + [VMEM] * 8,
        out_specs=VMEM,
        scratch_shapes=[pltpu.VMEM((96, D), BF16)],
        name="prepare",
    )(first, *rows, query_gain.reshape(1, HD), key_gain.reshape(1, HD))
    received = lax.all_to_all(message, ("yhi", "z"), 0, 0, tiled=True)
    query_pair, own = pl.pallas_call(
        repack,
        out_shape=(
            jax.ShapeDtypeStruct((SRC_ROWS, 2 * HD), BF16),
            jax.ShapeDtypeStruct((SRC_ROWS, 4 * HD), BF16),
        ),
        in_specs=[VMEM],
        out_specs=(VMEM, VMEM),
        name="repack",
    )(received)
    swap = [(0, 1), (1, 0)]
    across = lax.ppermute(own, "ylo", swap)
    beside = lax.ppermute(own, "core", swap)
    across_beside = lax.ppermute(across, "core", swap)
    message = pl.pallas_call(
        attend,
        out_shape=jax.ShapeDtypeStruct((SLOTS, BACK, HD), BF16),
        in_specs=[VMEM] * 5,
        out_specs=VMEM,
        scratch_shapes=[pltpu.VMEM((SRC_ROWS, HD), BF16)] * 2,
        name="attend",
    )(query_pair, own, beside, across, across_beside)
    received = lax.all_to_all(message, ("yhi", "z"), 0, 0, tiled=True)
    attended, attended_t = pl.pallas_call(
        unpack,
        out_shape=(jax.ShapeDtypeStruct((LOCAL, D), BF16),) * 2,
        in_specs=[VMEM],
        out_specs=(VMEM, VMEM),
        scratch_shapes=[pltpu.VMEM((16, D), BF16)],
        name="unpack",
    )(received)
    return attended.reshape(1, LOCAL, D), attended_t.reshape(1, LOCAL, D)


def solution(mesh):
    fine = Mesh(mesh.devices.reshape(4, 2, 8, 2, 4), ("yhi", "core", "z", "ylo", "x"))
    spec = P(("z", "ylo", "x"), ("yhi", "core"), None)
    return jax.shard_map(
        local,
        mesh=fine,
        in_specs=(spec,) * 6 + (P(), P()),
        out_specs=(spec, spec),
        check_vma=False,
    )
```

time: 285 us -> 108 us (0.38)
  waiting for transfers between devices: 111 us -> 13.9 us
  starting transfers between devices: 70.2 us -> 5.74 us
  local copies, waits for them, and re-layouts: 44.1 us -> 0.82 us
  blocking collectives: 25.3 us -> 68 us
  matrix products: 23.3 us -> 0 us
  Pallas kernels: 0 us -> 18.8 us
  other arithmetic: 6.41 us -> 0 us
    ppermute x15 -> x3, waiting for transfers between devices: 91.5 us -> 13.9 us  [the longest x1 11.9 us: local(): across = lax.ppermute(own, 'ylo', swap)]
    ppermute x15 -> x3, starting transfers between devices: 63 us -> 5.74 us  [the longest x1 1.92 us: local(): beside = lax.ppermute(own, 'core', swap)]
    all_to_all x1 -> x2, blocking collectives: 25.3 us -> 68 us  [local(): received = lax.all_to_all(message, ('yhi', 'z'), 0, 0, tiled=True)]
    dot_general x44 -> x0, matrix products: 23.3 us -> none  [the longest x8 11 us: absorb_segment(): jnp.einsum('qhd,khd->hqk', query_pair, key_pair, preferred_element_type=j...]
    unnamed x20 -> x6, local copies, waits for them, and re-layouts: 22.4 us -> 0.82 us
    all_to_all x1 -> x0, waiting for transfers between devices: 19.6 us -> none  [in_one_piece(): lax.all_to_all(both, axis, split_axis=split_dim, concat_axis=concat_dim,...]
    pallas_call x0 -> x4, Pallas kernels: none -> 18.8 us  [the longest x1 7.42 us: local(): pl.pallas_call(prepare, out_shape=jax.ShapeDtypeStruct((SLOTS, SEND, HD),...]
    concatenate x11 -> x0, local copies, waits for them, and re-layouts: 7.37 us -> none  [the longest x3 6.88 us: in_one_piece(): both = jnp.concatenate(arrays, axis=along)]
  transfers between devices with their start and end apart: 16 -> 3, of which waited for: 16 -> 2; matrix products, arithmetic and copies ran while one was open for 0% -> 0% of each run, Pallas kernels for 0% -> 0%
where the time goes in v1:
time: 108 us
  blocking collectives  68 us (63%)
  Pallas kernels  18.8 us (17%)
  waiting for transfers between devices  13.9 us (13%)
  starting transfers between devices  5.74 us (5%)
    all_to_all x2, blocking collectives, local(): received = lax.all_to_all(message, ('yhi', 'z'), 0, 0, tiled=True)  68 us
    ppermute x1, waiting for transfers between devices, local(): across = lax.ppermute(own, 'ylo', swap)  11.9 us
    pallas_call x1, Pallas kernels, local(): pl.pallas_call(prepare, out_shape=jax.ShapeDtypeStruct((SLOTS, SEND, HD),...  7.42 us
    pallas_call x1, Pallas kernels, local(): pl.pallas_call(attend, out_shape=jax.ShapeDtypeStruct((SLOTS, BACK, HD),...  7.24 us
    pallas_call x1, Pallas kernels, local(): pl.pallas_call(repack, out_shape=(jax.ShapeDtypeStruct((SRC_ROWS, 2 * HD)...  2.34 us
  transfers between devices with their start and end apart: 3, of which 2 were waited for; matrix products, arithmetic and copies ran while one was open for 0% of the time, Pallas kernels for 0%

profile of v1, /device:TPU:6, one launch (start us, length us, event | category | flops | bytes accessed | tf_op | source)
XLA Modules:
  0.0 107.9 jit_solution(4848527715076734874)
XLA Ops:
  0.6 7.4 %prepare.1 = bf16[32,112,128]{2,1,0:T(8,128)(2,1)} custom-call(s32[1]{0:T(128)} %bitcast.first, bf16[18,3072]{1,0:T(8,128)(2,1)} %bitcast.11, bf16[18,3072]{1,0:T(8,128)(2,1)} %bitcast.12, bf16[18,3072]{1,0:T(8,128)(2,1)} %bitcast.13, bf16[18,3072]{1,0:T(8,128)(2,1)} %bitcast.14, bf16[18,3072]{1,0:T(8,128)(2,1)} %bitcast.15, bf16[18,3072]{1,0:T(8,128)(2,1)} %bitcast.16, ...), custom_call_target="tpu_custom_call" | custom-call | tf_op jit(solution)/shard_map/prepare/pallas_call | solution.py:178
  8.1 44.1 %all_to_all.10.received = bf16[32,112,128]{2,1,0:T(8,128)(2,1)} all-to-all(bf16[32,112,128]{2,1,0:T(8,128)(2,1)} %prepare.1), channel_id=1, replica_groups=mesh['yhi'=4,'core'=2,'z'=8,'ylo'=2,'x'=4] {'yhi','z'}, dimensions={0} | all-to-all | bytes 1835008 | tf_op jit(solution)/shard_map/all_to_all | solution.py:186
  52.2 2.3 %repack.1 = (bf16[576,256]{1,0:T(8,128)(2,1)}, bf16[576,512]{1,0:T(8,128)(2,1)}) custom-call(bf16[32,112,128]{2,1,0:T(8,128)(2,1)} %all_to_all.10.received), custom_call_target="tpu_custom_call" | custom-call | tf_op jit(solution)/shard_map/repack/pallas_call | solution.py:187
  54.5 1.9 %collective-permute-start.1 = (bf16[576,512]{1,0:T(8,128)(2,1)}, bf16[576,512]{1,0:T(8,128)(2,1)S(1)}, u32[]{:S(2)}, u32[]{:S(2)}) collective-permute-start(bf16[576,512]{1,0:T(8,128)(2,1)} %get-tuple-element.7.kv0), channel_id=1, source_target_pairs={{0,4},{4,0},{1,5},{5,1},{2,6},{6,2},{3,7},{7,3},{8,12},{12,8},{9,1... | collective-permute-start | bytes 1769480 | tf_op jit(solution)/shard_map/ppermute | solution.py:198
  56.5 1.9 %collective-permute-start = (bf16[576,512]{1,0:T(8,128)(2,1)}, bf16[576,512]{1,0:T(8,128)(2,1)S(1)}, u32[]{:S(2)}, u32[]{:S(2)}) collective-permute-start(bf16[576,512]{1,0:T(8,128)(2,1)} %get-tuple-element.7.kv0), channel_id=1, source_target_pairs={{0,64},{64,0},{1,65},{65,1},{2,66},{66,2},{3,67},{67,3},{4,68},{68... | collective-permute-start | bytes 1769480 | tf_op jit(solution)/shard_map/ppermute | solution.py:199
  58.4 11.9 %collective-permute-done.1.kv2 = bf16[576,512]{1,0:T(8,128)(2,1)S(1)} collective-permute-done((bf16[576,512]{1,0:T(8,128)(2,1)}, bf16[576,512]{1,0:T(8,128)(2,1)S(1)}, u32[]{:S(2)}, u32[]{:S(2)}) %collective-permute-start.1) | collective-permute-done | bytes 589856 | tf_op jit(solution)/shard_map/ppermute | solution.py:198
  70.3 0.0 copy-start
  70.3 1.9 %collective-permute-start.2 = (bf16[576,512]{1,0:T(8,128)(2,1)S(1)}, bf16[576,512]{1,0:T(8,128)(2,1)S(1)}, u32[]{:S(2)}, u32[]{:S(2)}) collective-permute-start(bf16[576,512]{1,0:T(8,128)(2,1)S(1)} %collective-permute-done.1.kv2), channel_id=1, source_target_pairs={{0,64},{64,0},{1,65},{65,1},{2,66},{66,2},{3,67},{67,3},{4,68},{68... | collective-permute-start | bytes 1769480 | tf_op jit(solution)/shard_map/ppermute | solution.py:200
  72.2 0.0 collective-permute-done.kv1
  72.2 0.0 copy-start.1
  72.2 1.9 %collective-permute-done.2.kv3 = bf16[576,512]{1,0:T(8,128)(2,1)S(1)} collective-permute-done((bf16[576,512]{1,0:T(8,128)(2,1)S(1)}, bf16[576,512]{1,0:T(8,128)(2,1)S(1)}, u32[]{:S(2)}, u32[]{:S(2)}) %collective-permute-start.2) | collective-permute-done | bytes 589856 | tf_op jit(solution)/shard_map/ppermute | solution.py:200
  74.2 0.0 copy-start.2
  74.2 0.0 copy-done
  74.2 0.0 copy-done.1
  74.2 0.8 copy-done.2
  75.0 7.2 %attend.1 = bf16[32,40,128]{2,1,0:T(8,128)(2,1)} custom-call(bf16[576,256]{1,0:T(8,128)(2,1)} %get-tuple-element.6.query_pair, bf16[576,512]{1,0:T(8,128)(2,1)} %get-tuple-element.7.kv0, bf16[576,512]{1,0:T(8,128)(2,1)} %copy-done.1, bf16[576,512]{1,0:T(8,128)(2,1)} %copy-done, bf16[576,512]{1,0:T(8,128)(2,1)} %copy-done.2), custom_call_target="tpu_custom_call" | custom-call | tf_op jit(solution)/shard_map/attend/pallas_call | solution.py:201
  82.2 23.8 %all_to_all.11.received = bf16[32,40,128]{2,1,0:T(8,128)(2,1)} all-to-all(bf16[32,40,128]{2,1,0:T(8,128)(2,1)} %attend.1), channel_id=1, replica_groups=mesh['yhi'=4,'core'=2,'z'=8,'ylo'=2,'x'=4] {'yhi','z'}, dimensions={0} | all-to-all | bytes 655360 | tf_op jit(solution)/shard_map/all_to_all | solution.py:209
  106.1 1.8 %unpack.1 = (bf16[18,3072]{1,0:T(8,128)(2,1)}, bf16[18,3072]{1,0:T(8,128)(2,1)}) custom-call(bf16[32,40,128]{2,1,0:T(8,128)(2,1)} %all_to_all.11.received), custom_call_target="tpu_custom_call" | custom-call | tf_op jit(solution)/shard_map/unpack/pallas_call | solution.py:210
Async XLA Ops:
  54.5 15.8 %collective-permute-start.1 = (bf16[576,512]{1,0:T(8,128)(2,1)}, bf16[576,512]{1,0:T(8,128)(2,1)S(1)}, u32[]{:S(2)}, u32[]{:S(2)}) collective-permute-start(bf16[576,512]{1,0:T(8,128)(2,1)} %get-tuple-element.7.kv0), channel_id=1, source_target_pairs={{0,4},{4,0},{1,5},{5,1},{2,6},{6,2},{3,7},{7,3},{8,12},{12,8},{9,1... | collective-permute-start | bytes 1769480 | tf_op jit(solution)/shard_map/ppermute | solution.py:198
  56.5 15.8 %collective-permute-start = (bf16[576,512]{1,0:T(8,128)(2,1)}, bf16[576,512]{1,0:T(8,128)(2,1)S(1)}, u32[]{:S(2)}, u32[]{:S(2)}) collective-permute-start(bf16[576,512]{1,0:T(8,128)(2,1)} %get-tuple-element.7.kv0), channel_id=1, source_target_pairs={{0,64},{64,0},{1,65},{65,1},{2,66},{66,2},{3,67},{67,3},{4,68},{68... | collective-permute-start | bytes 1769480 | tf_op jit(solution)/shard_map/ppermute | solution.py:199
  70.3 3.9 %copy-start = (bf16[576,512]{1,0:T(8,128)(2,1)}, bf16[576,512]{1,0:T(8,128)(2,1)S(1)}, u32[]{:S(2)}) copy-start(bf16[576,512]{1,0:T(8,128)(2,1)S(1)} %collective-permute-done.1.kv2) | copy-start | bytes 1769476
  70.3 3.9 %collective-permute-start.2 = (bf16[576,512]{1,0:T(8,128)(2,1)S(1)}, bf16[576,512]{1,0:T(8,128)(2,1)S(1)}, u32[]{:S(2)}, u32[]{:S(2)}) collective-permute-start(bf16[576,512]{1,0:T(8,128)(2,1)S(1)} %collective-permute-done.1.kv2), channel_id=1, source_target_pairs={{0,64},{64,0},{1,65},{65,1},{2,66},{66,2},{3,67},{67,3},{4,68},{68... | collective-permute-start | bytes 1769480 | tf_op jit(solution)/shard_map/ppermute | solution.py:200
  72.2 2.0 %copy-start.1 = (bf16[576,512]{1,0:T(8,128)(2,1)}, bf16[576,512]{1,0:T(8,128)(2,1)S(1)}, u32[]{:S(2)}) copy-start(bf16[576,512]{1,0:T(8,128)(2,1)S(1)} %collective-permute-done.kv1) | copy-start | bytes 1769476
  74.2 0.8 copy-start.2

commit v2 on v1

--- a/solution.py
+++ b/solution.py
@@ -113,46 +113,66 @@
 BQ = 192
 
 
-def attend(query_pair, kv0, kv1, kv2, kv3, out, attended, attended_t):
-    blocks = (kv0, kv1, kv2, kv3)
-    for b in range(SRC_ROWS // BQ):
-        at = slice(b * BQ, (b + 1) * BQ)
-        pair = query_pair[at, :]
-        hat = query_pair[at, HD:]
-        scores = [
-            lax.dot_general(hat, kv[:, 0:HD], TRANSPOSED, preferred_element_type=F32) for kv in blocks
-        ]
-        peak = jnp.max(scores[0], axis=1, keepdims=True)
-        for s in scores[1:]:
-            peak = jnp.maximum(peak, jnp.max(s, axis=1, keepdims=True))
-        total = drift = both = extra = 0.0
-        for s, kv in zip(scores, blocks):
-            weights = jnp.exp2((s - peak) * (SCALE * math.log2(math.e)))
-            moved = lax.dot_general(pair, kv[:, 0 : 2 * HD], TRANSPOSED, preferred_element_type=F32)
-            product = weights * (moved * SCALE)
-            total = total + jnp.sum(weights, axis=1, keepdims=True)
-            drift = drift + jnp.sum(product, axis=1, keepdims=True)
-            both = both + jnp.dot(
-                weights.astype(BF16), kv[:, 2 * HD : 4 * HD], preferred_element_type=F32
-            )
-            extra = extra + jnp.dot(
-                product.astype(BF16), kv[:, 2 * HD : 3 * HD], preferred_element_type=F32
-            )
-        summed = both[:, :HD]
-        summed_dot = both[:, HD:] + extra
+def absorb(query_pair, blocks, at, state):
+    pair = query_pair[at, :]
+    hat = query_pair[at, HD:]
+    scores = [lax.dot_general(hat, kv[:, 0:HD], TRANSPOSED, preferred_element_type=F32) for kv in blocks]
+    peak = None if state is None else state[0]
+    for s in scores:
+        top = jnp.max(s, axis=1, keepdims=True)
+        peak = top if peak is None else jnp.maximum(peak, top)
+    total = drift = both = extra = 0.0
+    for s, kv in zip(scores, blocks):
+        weights = jnp.exp2((s - peak) * (SCALE * math.log2(math.e)))
+        moved = lax.dot_general(pair, kv[:, 0 : 2 * HD], TRANSPOSED, preferred_element_type=F32)
+        product = weights * (moved * SCALE)
+        total = total + jnp.sum(weights, axis=1, keepdims=True)
+        drift = drift + jnp.sum(product, axis=1, keepdims=True)
+        both = both + jnp.dot(weights.astype(BF16), kv[:, 2 * HD : 4 * HD], preferred_element_type=F32)
+        extra = extra + jnp.dot(product.astype(BF16), kv[:, 2 * HD : 3 * HD], preferred_element_type=F32)
+    summed = both[:, :HD]
+    summed_dot = both[:, HD:] + extra
+    if state is None:
+        return peak, total, drift, summed, summed_dot
+    rescale = jnp.exp2((state[0] - peak) * (SCALE * math.log2(math.e)))
+    old = [part * rescale for part in state[1:]]
+    return peak, old[0] + total, old[1] + drift, old[2] + summed, old[3] + summed_dot
+
+
+QUERY_BLOCKS = [slice(b, b + BQ) for b in range(0, SRC_ROWS, BQ)]
+
+
+def attend_first(query_pair, kv0, kv1, *state):
+    for at in QUERY_BLOCKS:
+        for ref, part in zip(state, absorb(query_pair, (kv0, kv1), at, None)):
+            ref[at, :] = part
+
+
+def attend_next(query_pair, kv, *states):
+    before, after = states[:5], states[5:]
+    for at in QUERY_BLOCKS:
+        for ref, part in zip(after, absorb(query_pair, (kv,), at, [ref[at, :] for ref in before])):
+            ref[at, :] = part
+
+
+def attend_last(query_pair, kv, *rest):
+    before, (out, attended, attended_t) = rest[:5], rest[5:]
+    for at in QUERY_BLOCKS:
+        state = absorb(query_pair, (kv,), at, [ref[at, :] for ref in before])
+        _, total, drift, summed, summed_dot = state
         attended[at, :] = (summed / total).astype(BF16)
         attended_t[at, :] = ((summed_dot - drift / total * summed) / total).astype(BF16)
     for source in range(SLOTS):
         at = slice(16 * source, 16 * source + 16)
         out[source, 0:16, :] = attended[at, :]
         out[source, 16:32, :] = attended_t[at, :]
-    rest = jnp.concatenate([attended[512:576, :], attended_t[512:576, :]], axis=0)
+    tail = jnp.concatenate([attended[512:576, :], attended_t[512:576, :]], axis=0)
     pick = one_hot(
         (256, 128),
         lambda r: (r >> 3) * 2 + (r & 1) + jnp.where((r & 2) > 0, 64, 0),
         lambda r: (r & 7) < 4,
     )
-    slabs = jnp.dot(pick, rest, preferred_element_type=F32).astype(BF16)
+    slabs = jnp.dot(pick, tail, preferred_element_type=F32).astype(BF16)
     out[:, 32:40, :] = slabs.reshape(SLOTS, 8, HD)
 
 
@@ -170,51 +190,58 @@
     attended_t[16:18, :] = rest[8:10].astype(BF16)
 
 
+def call(kernel, outs, scratch=(), on_chip=True, kept=True, keys=0):
+    make = pltpu.VMEM if kept else jax.ShapeDtypeStruct
+    shapes = tuple(make(shape, dtype) for shape, dtype in outs)
+    one = len(shapes) == 1
+
+    def run(*args):
+        if on_chip:
+            specs = [VMEM] * len(args)
+            args = [pltpu.with_memory_space_constraint(a, pltpu.VMEM) for a in args]
+        else:
+            specs = [SMEM] + [VMEM] * (len(args) - 1)
+        return pl.pallas_call(
+            kernel,
+            out_shape=shapes[0] if one else shapes,
+            in_specs=specs,
+            out_specs=VMEM if one else (VMEM,) * len(shapes),
+            scratch_shapes=list(scratch),
+            cost_estimate=pl.CostEstimate(
+                flops=16 * SRC_ROWS * HD * keys, transcendentals=SRC_ROWS * keys, bytes_accessed=10**6
+            ),
+            compiler_params=pltpu.CompilerParams(vmem_limit_bytes=24 * 2**20),
+            name=kernel.__name__,
+        )(*args)
+
+    return run
+
+
 def local(query, key, value, query_t, key_t, value_t, query_gain, key_gain):
     place = lax.axis_index("z") * 2 + lax.axis_index("ylo")
     share = lax.axis_index("yhi") * 2 + lax.axis_index("core")
     first = (place * ROWS + share * LOCAL).reshape(1)
     rows = [a.reshape(LOCAL, D) for a in (query, key, value, query_t, key_t, value_t)]
-    message = pl.pallas_call(
-        prepare,
-        out_shape=jax.ShapeDtypeStruct((SLOTS, SEND, HD), BF16),
-        in_specs=[SMEM] + [VMEM] * 8,
-        out_specs=VMEM,
-        scratch_shapes=[pltpu.VMEM((96, D), BF16)],
-        name="prepare",
-    )(first, *rows, query_gain.reshape(1, HD), key_gain.reshape(1, HD))
+    message = call(prepare, [((SLOTS, SEND, HD), BF16)], [pltpu.VMEM((96, D), BF16)], on_chip=False)(
+        first, *rows, query_gain.reshape(1, HD), key_gain.reshape(1, HD)
+    )
     received = lax.all_to_all(message, ("yhi", "z"), 0, 0, tiled=True)
-    query_pair, own = pl.pallas_call(
-        repack,
-        out_shape=(
-            jax.ShapeDtypeStruct((SRC_ROWS, 2 * HD), BF16),
-            jax.ShapeDtypeStruct((SRC_ROWS, 4 * HD), BF16),
-        ),
-        in_specs=[VMEM],
-        out_specs=(VMEM, VMEM),
-        name="repack",
-    )(received)
+    query_pair, own = call(repack, [((SRC_ROWS, 2 * HD), BF16), ((SRC_ROWS, 4 * HD), BF16)])(received)
     swap = [(0, 1), (1, 0)]
     across = lax.ppermute(own, "ylo", swap)
     beside = lax.ppermute(own, "core", swap)
+    state_shapes = [((SRC_ROWS, 1), F32)] * 3 + [((SRC_ROWS, HD), F32)] * 2
+    state = call(attend_first, state_shapes, keys=2 * SRC_ROWS)(query_pair, own, beside)
+    across, *state = lax.optimization_barrier((across, *state))
     across_beside = lax.ppermute(across, "core", swap)
-    message = pl.pallas_call(
-        attend,
-        out_shape=jax.ShapeDtypeStruct((SLOTS, BACK, HD), BF16),
-        in_specs=[VMEM] * 5,
-        out_specs=VMEM,
-        scratch_shapes=[pltpu.VMEM((SRC_ROWS, HD), BF16)] * 2,
-        name="attend",
-    )(query_pair, own, beside, across, across_beside)
+    state = call(attend_next, state_shapes, keys=SRC_ROWS)(query_pair, across, *state)
+    message = call(attend_last, [((SLOTS, BACK, HD), BF16)], [pltpu.VMEM((SRC_ROWS, HD), BF16)] * 2, keys=SRC_ROWS)(
+        query_pair, across_beside, *state
+    )
     received = lax.all_to_all(message, ("yhi", "z"), 0, 0, tiled=True)
-    attended, attended_t = pl.pallas_call(
-        unpack,
-        out_shape=(jax.ShapeDtypeStruct((LOCAL, D), BF16),) * 2,
-        in_specs=[VMEM],
-        out_specs=(VMEM, VMEM),
-        scratch_shapes=[pltpu.VMEM((16, D), BF16)],
-        name="unpack",
-    )(received)
+    attended, attended_t = call(unpack, [((LOCAL, D), BF16)] * 2, [pltpu.VMEM((16, D), BF16)], kept=False)(
+        received
+    )
     return attended.reshape(1, LOCAL, D), attended_t.reshape(1, LOCAL, D)
 
 

time: 108 us -> 106 us (0.981)
  Pallas kernels: 18.8 us -> 13 us
  local copies, waits for them, and re-layouts: 0.82 us -> 6.11 us
  blocking collectives: 68 us -> 66.3 us
    pallas_call x4 -> x6, Pallas kernels: 18.8 us -> 13 us  [run(): pl.pallas_call(kernel, out_shape=shapes[0] if one else shapes, in_specs=s...]
    unnamed x6 -> x16, local copies, waits for them, and re-layouts: 0.82 us -> 6.11 us
    ppermute x1, waiting for transfers between devices: 1.95 us -> 0.04 us  [local(): across_beside = lax.ppermute(across, 'core', swap)]
    all_to_all x2, blocking collectives: 68 us -> 66.3 us  [local(): received = lax.all_to_all(message, ('yhi', 'z'), 0, 0, tiled=True)]
    ppermute x1, waiting for transfers between devices: 11.9 us -> 13.2 us  [local(): across = lax.ppermute(own, 'ylo', swap)]
  transfers between devices with their start and end apart: 3 -> 3, of which waited for: 2 -> 1; matrix products, arithmetic and copies ran while one was open for 0% -> 0% of each run, Pallas kernels for 0% -> 4%
where the time goes in v2:
time: 106 us; the launch traced here: 105 us
  blocking collectives  66.3 us (63%)
  waiting for transfers between devices  13.3 us (13%)
  Pallas kernels  13 us (12%)
  local copies, waits for them, and re-layouts  6.11 us (6%)
  starting transfers between devices  5.75 us (5%)
    all_to_all x2, blocking collectives, local(): received = lax.all_to_all(message, ('yhi', 'z'), 0, 0, tiled=True)  66.3 us
    ppermute x1, waiting for transfers between devices, local(): across = lax.ppermute(own, 'ylo', swap)  13.2 us
    pallas_call x6, Pallas kernels, run(): pl.pallas_call(kernel, out_shape=shapes[0] if one else shapes, in_specs=s...  13 us
    unnamed x16, local copies, waits for them, and re-layouts  6.11 us
  transfers between devices with their start and end apart: 3, of which 1 were waited for; matrix products, arithmetic and copies ran while one was open for 0% of the time, Pallas kernels for 4%

profile of v2, /device:TPU:6, one launch (start us, length us, event | category | flops | bytes accessed | tf_op | source)
XLA Modules:
  0.0 105.1 jit_solution(50680369749112468)
XLA Ops:
  0.6 0.0 copy-start.6
  0.7 0.0 copy-start.7
  0.7 0.6 copy-done.6
  1.3 0.0 copy-done.7
  1.3 0.0 copy-start
  1.3 0.9 copy-done
  2.2 0.0 copy-start.1
  2.2 0.9 copy-done.1
  3.1 0.0 copy-start.2
  3.1 0.9 copy-done.2
  4.0 0.0 copy-start.3
  4.0 0.9 copy-done.3
  5.0 0.0 copy-start.4
  5.0 0.9 copy-done.4
  5.9 0.0 copy-start.5
  5.9 0.9 copy-done.5
  6.8 5.2 %prepare.1 = bf16[32,112,128]{2,1,0:T(8,128)(2,1)S(1)} custom-call(s32[1]{0:T(128)} %bitcast.first, bf16[18,3072]{1,0:T(8,128)(2,1)S(1)} %bitcast.11, bf16[18,3072]{1,0:T(8,128)(2,1)S(1)} %bitcast.12, bf16[18,3072]{1,0:T(8,128)(2,1)S(1)} %bitcast.13, bf16[18,3072]{1,0:T(8,128)(2,1)S(1)} %bitcast.14, bf16[18,3072]{1,0:T(8,128)(2,1)S(1)} %bitcast.15, ...), custom_call_target="tpu_custom_call" | custom-call | bytes 1000000 | tf_op jit(solution)/shard_map/prepare/pallas_call | solution.py:204
  12.0 43.8 %all_to_all.10.received = bf16[32,112,128]{2,1,0:T(8,128)(2,1)S(1)} all-to-all(bf16[32,112,128]{2,1,0:T(8,128)(2,1)S(1)} %prepare.1), channel_id=1, replica_groups=mesh['yhi'=4,'core'=2,'z'=8,'ylo'=2,'x'=4] {'yhi','z'}, dimensions={0} | all-to-all | bytes 1835008 | tf_op jit(solution)/shard_map/all_to_all | solution.py:228
  55.8 0.4 repack.1
  56.2 1.9 %collective-permute-start.1 = (bf16[576,512]{1,0:T(8,128)(2,1)S(1)}, bf16[576,512]{1,0:T(8,128)(2,1)S(1)}, u32[]{:S(2)}, u32[]{:S(2)}) collective-permute-start(bf16[576,512]{1,0:T(8,128)(2,1)S(1)} %get-tuple-element.23.kv0), channel_id=1, source_target_pairs={{0,64},{64,0},{1,65},{65,1},{2,66},{66,2},{3,67},{67,3},{4,68},{68... | collective-permute-start | bytes 1769480 | tf_op jit(solution)/shard_map/ppermute | solution.py:232
  58.2 1.9 %collective-permute-start = (bf16[576,512]{1,0:T(8,128)(2,1)S(1)}, bf16[576,512]{1,0:T(8,128)(2,1)S(1)}, u32[]{:S(2)}, u32[]{:S(2)}) collective-permute-start(bf16[576,512]{1,0:T(8,128)(2,1)S(1)} %get-tuple-element.23.kv0), channel_id=1, source_target_pairs={{0,4},{4,0},{1,5},{5,1},{2,6},{6,2},{3,7},{7,3},{8,12},{12,8},{9,1... | collective-permute-start | bytes 1769480 | tf_op jit(solution)/shard_map/ppermute | solution.py:231
  60.1 0.0 collective-permute-done.1.kv1
  60.1 2.5 %attend_first.1 = (f32[576,1]{1,0:T(8,128)S(1)}, f32[576,1]{1,0:T(8,128)S(1)}, f32[576,1]{1,0:T(8,128)S(1)}, f32[576,128]{1,0:T(8,128)S(1)}, f32[576,128]{1,0:T(8,128)S(1)}) custom-call(bf16[576,256]{1,0:T(8,128)(2,1)S(1)} %get-tuple-element.22.query_pair, bf16[576,512]{1,0:T(8,128)(2,1)S(1)} %get-tuple-element.23.kv0, ...), custom_call_target="tpu_custom_call" | custom-call | flops 1358954496 | bytes 1000000 | tf_op jit(solution)/shard_map/attend_first/pallas_call | solution.py:204
  62.6 13.2 %collective-permute-done.kv = bf16[576,512]{1,0:T(8,128)(2,1)S(1)} collective-permute-done((bf16[576,512]{1,0:T(8,128)(2,1)S(1)}, bf16[576,512]{1,0:T(8,128)(2,1)S(1)}, u32[]{:S(2)}, u32[]{:S(2)}) %collective-permute-start) | collective-permute-done | bytes 589856 | tf_op jit(solution)/shard_map/ppermute | solution.py:231
  75.8 1.9 %collective-permute-start.2 = (bf16[576,512]{1,0:T(8,128)(2,1)S(1)}, bf16[576,512]{1,0:T(8,128)(2,1)S(1)}, u32[]{:S(2)}, u32[]{:S(2)}) collective-permute-start(bf16[576,512]{1,0:T(8,128)(2,1)S(1)} %collective-permute-done.kv), channel_id=1, source_target_pairs={{0,64},{64,0},{1,65},{65,1},{2,66},{66,2},{3,67},{67,3},{4,68},{68... | collective-permute-start | bytes 1769480 | tf_op jit(solution)/shard_map/ppermute | solution.py:236
  77.7 1.9 %attend_next.1 = (f32[576,1]{1,0:T(8,128)S(1)}, f32[576,1]{1,0:T(8,128)S(1)}, f32[576,1]{1,0:T(8,128)S(1)}, f32[576,128]{1,0:T(8,128)S(1)}, f32[576,128]{1,0:T(8,128)S(1)}) custom-call(bf16[576,256]{1,0:T(8,128)(2,1)S(1)} %get-tuple-element.22.query_pair, bf16[576,512]{1,0:T(8,128)(2,1)S(1)} %collective-permute-done.kv, ...), custom_call_target="tpu_custom_call" | custom-call | flops 679477248 | bytes 1000000 | tf_op jit(solution)/shard_map/attend_next/pallas_call | solution.py:204
  79.6 0.0 collective-permute-done.2.kv
  79.7 2.1 %attend_last.1 = bf16[32,40,128]{2,1,0:T(8,128)(2,1)S(1)} custom-call(bf16[576,256]{1,0:T(8,128)(2,1)S(1)} %get-tuple-element.22.query_pair, bf16[576,512]{1,0:T(8,128)(2,1)S(1)} %collective-permute-done.2.kv, f32[576,1]{1,0:T(8,128)S(1)} %get-tuple-element.35.rest_0_, f32[576,1]{1,0:T(8,128)S(1)} %get-tuple-element.36.rest_1_, ...), custom_call_target="tpu_custom_call" | custom-call | flops 679477248 | bytes 1000000 | tf_op jit(solution)/shard_map/attend_last/pallas_call | solution.py:204
  81.8 22.4 %all_to_all.11.received = bf16[32,40,128]{2,1,0:T(8,128)(2,1)S(1)} all-to-all(bf16[32,40,128]{2,1,0:T(8,128)(2,1)S(1)} %attend_last.1), channel_id=1, replica_groups=mesh['yhi'=4,'core'=2,'z'=8,'ylo'=2,'x'=4] {'yhi','z'}, dimensions={0} | all-to-all | bytes 655360 | tf_op jit(solution)/shard_map/all_to_all | solution.py:241
  104.2 0.9 unpack.1
Async XLA Ops:
  0.6 0.7 copy-start.6
  0.7 0.7 copy-start.7
  1.3 0.9 copy-start
  2.2 0.9 copy-start.1
  3.1 0.9 copy-start.2
  4.0 0.9 copy-start.3
  5.0 0.9 copy-start.4
  5.9 0.9 copy-start.5
  56.2 3.9 %collective-permute-start.1 = (bf16[576,512]{1,0:T(8,128)(2,1)S(1)}, bf16[576,512]{1,0:T(8,128)(2,1)S(1)}, u32[]{:S(2)}, u32[]{:S(2)}) collective-permute-start(bf16[576,512]{1,0:T(8,128)(2,1)S(1)} %get-tuple-element.23.kv0), channel_id=1, source_target_pairs={{0,64},{64,0},{1,65},{65,1},{2,66},{66,2},{3,67},{67,3},{4,68},{68... | collective-permute-start | bytes 1769480 | tf_op jit(solution)/shard_map/ppermute | solution.py:232
  58.2 17.6 %collective-permute-start = (bf16[576,512]{1,0:T(8,128)(2,1)S(1)}, bf16[576,512]{1,0:T(8,128)(2,1)S(1)}, u32[]{:S(2)}, u32[]{:S(2)}) collective-permute-start(bf16[576,512]{1,0:T(8,128)(2,1)S(1)} %get-tuple-element.23.kv0), channel_id=1, source_target_pairs={{0,4},{4,0},{1,5},{5,1},{2,6},{6,2},{3,7},{7,3},{8,12},{12,8},{9,1... | collective-permute-start | bytes 1769480 | tf_op jit(solution)/shard_map/ppermute | solution.py:231
  75.8 3.9 %collective-permute-start.2 = (bf16[576,512]{1,0:T(8,128)(2,1)S(1)}, bf16[576,512]{1,0:T(8,128)(2,1)S(1)}, u32[]{:S(2)}, u32[]{:S(2)}) collective-permute-start(bf16[576,512]{1,0:T(8,128)(2,1)S(1)} %collective-permute-done.kv), channel_id=1, source_target_pairs={{0,64},{64,0},{1,65},{65,1},{2,66},{66,2},{3,67},{67,3},{4,68},{68... | collective-permute-start | bytes 1769480 | tf_op jit(solution)/shard_map/ppermute | solution.py:236

commit v3 on v2

--- a/solution.py
+++ b/solution.py
@@ -18,6 +18,7 @@
 MAIN = 16
 SLOTS = 32
 SRC_ROWS = 576
+EARLY = 320
 SEND = 112
 BACK = 40
 EPSILON = 1e-06
@@ -28,6 +29,7 @@
 
 VMEM = pl.BlockSpec(memory_space=pltpu.VMEM)
 SMEM = pl.BlockSpec(memory_space=pltpu.SMEM)
+HBM = pl.BlockSpec(memory_space=pltpu.HBM)
 
 
 def slot_of(head):
@@ -44,7 +46,15 @@
     return jnp.where((column == column_of_row(row)) & valid(row), 1.0, 0.0).astype(BF16)
 
 
-def prepare(first, query, key, value, query_t, key_t, value_t, query_gain, key_gain, out, tails):
+def prepare(first, *refs):
+    sources, (out, tails), buffers, arrival = refs[:8], refs[8:10], refs[10:18], refs[18]
+    copies = [
+        pltpu.make_async_copy(source, buffer, arrival.at[i])
+        for i, (source, buffer) in enumerate(zip(sources, buffers))
+    ]
+    for copy in copies:
+        copy.start()
+    query, key, value, query_t, key_t, value_t, query_gain, key_gain = buffers
     token = first[0] + lax.broadcasted_iota(jnp.int32, (LOCAL, HD), 0)
     lane = lax.broadcasted_iota(jnp.int32, (LOCAL, HD), 1)
     patch = jnp.maximum(token - TXT, 0)
@@ -57,34 +67,38 @@
     frequency = jnp.exp(-math.log(THETA) * (step * (2.0 / 56.0)))
     angle = jnp.where(pair < 8, 0.0, jnp.where(of_row, row_id, column_id) * frequency)
     cosine = jnp.cos(angle)
-    sine = jnp.sin(angle)
     even = (lane & 1) == 0
-    sine_even = jnp.where(even, -sine, 0.0)
-    sine_odd = jnp.where(even, 0.0, sine)
-
-    def rotate(x):
-        after = pltpu.roll(x, HD - 1, 1)
-        before = pltpu.roll(x, 1, 1)
-        return (x * cosine + after * sine_even + before * sine_odd).astype(BF16)
-
-    def normalize(raw, tangent, gain):
+    sine = jnp.where(even, -jnp.sin(angle), jnp.sin(angle))
+
+    def turned(gain):
+        wide = jnp.broadcast_to(gain, (LOCAL, HD))
+        partner = jnp.where(even, pltpu.roll(wide, HD - 1, 1), pltpu.roll(wide, 1, 1))
+        return wide * cosine, partner * sine
+
+    exchange = one_hot((HD, HD), lambda r: r ^ 1, lambda r: r >= 0)
+
+    def normalize(raw, tangent, own, other):
         x = raw.astype(F32)
         u = tangent.astype(F32)
         inverse = lax.rsqrt(jnp.mean(x * x, axis=1, keepdims=True) + EPSILON)
         coupling = jnp.mean(x * u, axis=1, keepdims=True)
-        xr = x * inverse
-        normed = xr * gain
-        dotted = gain * (u * inverse - xr * (inverse * inverse * coupling))
-        return rotate(normed), rotate(dotted)
+        x_turned = x * own + jnp.dot(raw, exchange, preferred_element_type=F32) * other
+        u_turned = u * own + jnp.dot(tangent, exchange, preferred_element_type=F32) * other
+        dotted = u_turned * inverse - x_turned * (inverse * inverse * inverse * coupling)
+        return (x_turned * inverse).astype(BF16), dotted.astype(BF16)
 
     tails[...] = jnp.zeros_like(tails)
-    qg = query_gain[...]
-    kg = key_gain[...]
+    for slot in range(HEADS, SLOTS):
+        out[slot] = jnp.zeros((SEND, HD), BF16)
+    for copy in copies:
+        copy.wait()
+    of_query = turned(query_gain[...])
+    of_key = turned(key_gain[...])
     for head in range(HEADS):
         here = lanes(head)
         slot = slot_of(head)
-        q_hat, q_dot = normalize(query[:, here], query_t[:, here], qg)
-        k_hat, k_dot = normalize(key[:, here], key_t[:, here], kg)
+        q_hat, q_dot = normalize(query[:, here], query_t[:, here], *of_query)
+        k_hat, k_dot = normalize(key[:, here], key_t[:, here], *of_key)
         parts = (q_hat, q_dot, k_hat, k_dot, value[:, here], value_t[:, here])
         for t, part in enumerate(parts):
             out[slot, 16 * t : 16 * t + 16, :] = part[:MAIN]
@@ -93,20 +107,28 @@
     slab = jnp.dot(pick, tails[...], preferred_element_type=F32).astype(BF16)
     for head in range(HEADS):
         out[slot_of(head), 96:112, :] = slab[:, lanes(head)]
-    for slot in range(HEADS, SLOTS):
-        out[slot] = jnp.zeros((SEND, HD), BF16)
-
-
-def repack(received, query_pair, key_value):
-    places = ((query_pair, 128), (query_pair, 0)) + tuple((key_value, 128 * j) for j in range(4))
+
+
+def repack(received, query_pair, own, early, late):
     for source in range(SLOTS):
-        for t, (ref, at) in enumerate(places):
-            ref[16 * source : 16 * source + 16, at : at + HD] = received[source, 16 * t : 16 * t + 16, :]
+        row = 16 * source
+        key_value, row_there = (early, row) if row < EARLY else (late, row - EARLY)
+        for t, at in enumerate((128, 0, 0, 128, 256, 384)):
+            part = received[source, 16 * t : 16 * t + 16, :]
+            if t < 2:
+                query_pair[row : row + 16, at : at + HD] = part
+            else:
+                own[row : row + 16, at : at + HD] = part
+                key_value[row_there : row_there + 16, at : at + HD] = part
     slabs = received[:, 96:112, :].reshape(SLOTS * 16, HD)
-    for t, (ref, at) in enumerate(places):
+    for t, at in enumerate((128, 0, 0, 128, 256, 384)):
         pick = one_hot((64, 512), lambda r: (r >> 1) * 16 + 2 * t + (r & 1), lambda r: r >= 0)
-        rest = jnp.dot(pick, slabs, preferred_element_type=F32).astype(BF16)
-        ref[512:576, at : at + HD] = rest
+        part = jnp.dot(pick, slabs, preferred_element_type=F32).astype(BF16)
+        if t < 2:
+            query_pair[512:576, at : at + HD] = part
+        else:
+            own[512:576, at : at + HD] = part
+            late[512 - EARLY : 576 - EARLY, at : at + HD] = part
 
 
 TRANSPOSED = (((1,), (1,)), ((), ()))
@@ -142,16 +164,17 @@
 QUERY_BLOCKS = [slice(b, b + BQ) for b in range(0, SRC_ROWS, BQ)]
 
 
-def attend_first(query_pair, kv0, kv1, *state):
+def attend_first(query_pair, *rest):
+    blocks, state = rest[:-5], rest[-5:]
     for at in QUERY_BLOCKS:
-        for ref, part in zip(state, absorb(query_pair, (kv0, kv1), at, None)):
+        for ref, part in zip(state, absorb(query_pair, blocks, at, None)):
             ref[at, :] = part
 
 
-def attend_next(query_pair, kv, *states):
-    before, after = states[:5], states[5:]
+def attend_next(query_pair, *rest):
+    blocks, before, after = rest[:-10], rest[-10:-5], rest[-5:]
     for at in QUERY_BLOCKS:
-        for ref, part in zip(after, absorb(query_pair, (kv,), at, [ref[at, :] for ref in before])):
+        for ref, part in zip(after, absorb(query_pair, blocks, at, [ref[at, :] for ref in before])):
             ref[at, :] = part
 
 
@@ -190,28 +213,27 @@
     attended_t[16:18, :] = rest[8:10].astype(BF16)
 
 
-def call(kernel, outs, scratch=(), on_chip=True, kept=True, keys=0):
+def call(kernel, outs, scratch=(), specs=None, kept=True, keys=0):
     make = pltpu.VMEM if kept else jax.ShapeDtypeStruct
     shapes = tuple(make(shape, dtype) for shape, dtype in outs)
     one = len(shapes) == 1
 
     def run(*args):
-        if on_chip:
-            specs = [VMEM] * len(args)
-            args = [pltpu.with_memory_space_constraint(a, pltpu.VMEM) for a in args]
-        else:
-            specs = [SMEM] + [VMEM] * (len(args) - 1)
+        places = specs or [VMEM] * len(args)
+        args = [
+            a if spec is SMEM else pltpu.with_memory_space_constraint(a, spec.memory_space)
+            for a, spec in zip(args, places)
+        ]
         return pl.pallas_call(
             kernel,
             out_shape=shapes[0] if one else shapes,
-            in_specs=specs,
+            in_specs=places,
             out_specs=VMEM if one else (VMEM,) * len(shapes),
             scratch_shapes=list(scratch),
             cost_estimate=pl.CostEstimate(
                 flops=16 * SRC_ROWS * HD * keys, transcendentals=SRC_ROWS * keys, bytes_accessed=10**6
             ),
             compiler_params=pltpu.CompilerParams(vmem_limit_bytes=24 * 2**20),
-            name=kernel.__name__,
         )(*args)
 
     return run
@@ -222,22 +244,40 @@
     share = lax.axis_index("yhi") * 2 + lax.axis_index("core")
     first = (place * ROWS + share * LOCAL).reshape(1)
     rows = [a.reshape(LOCAL, D) for a in (query, key, value, query_t, key_t, value_t)]
-    message = call(prepare, [((SLOTS, SEND, HD), BF16)], [pltpu.VMEM((96, D), BF16)], on_chip=False)(
-        first, *rows, query_gain.reshape(1, HD), key_gain.reshape(1, HD)
-    )
+    landing = [pltpu.VMEM((LOCAL, D), BF16)] * 6 + [pltpu.VMEM((1, HD), F32)] * 2
+    landing.append(pltpu.SemaphoreType.DMA((8,)))
+    message = call(
+        prepare,
+        [((SLOTS, SEND, HD), BF16)],
+        [pltpu.VMEM((96, D), BF16)] + landing,
+        specs=[SMEM] + [HBM] * 8,
+    )(first, *rows, query_gain.reshape(1, HD), key_gain.reshape(1, HD))
     received = lax.all_to_all(message, ("yhi", "z"), 0, 0, tiled=True)
-    query_pair, own = call(repack, [((SRC_ROWS, 2 * HD), BF16), ((SRC_ROWS, 4 * HD), BF16)])(received)
-    swap = [(0, 1), (1, 0)]
-    across = lax.ppermute(own, "ylo", swap)
-    beside = lax.ppermute(own, "core", swap)
+    query_pair, own, early, late = call(
+        repack,
+        [((SRC_ROWS, 2 * HD), BF16)] + [((n, 4 * HD), BF16) for n in (SRC_ROWS, EARLY, SRC_ROWS - EARLY)],
+    )(received)
     state_shapes = [((SRC_ROWS, 1), F32)] * 3 + [((SRC_ROWS, HD), F32)] * 2
-    state = call(attend_first, state_shapes, keys=2 * SRC_ROWS)(query_pair, own, beside)
-    across, *state = lax.optimization_barrier((across, *state))
-    across_beside = lax.ppermute(across, "core", swap)
-    state = call(attend_next, state_shapes, keys=SRC_ROWS)(query_pair, across, *state)
-    message = call(attend_last, [((SLOTS, BACK, HD), BF16)], [pltpu.VMEM((SRC_ROWS, HD), BF16)] * 2, keys=SRC_ROWS)(
-        query_pair, across_beside, *state
-    )
+
+    def swapped(block, axis):
+        return lax.ppermute(block, axis, [(0, 1), (1, 0)])
+
+    early_across = swapped(early, "ylo")
+    late_across = swapped(late, "ylo")
+    own_beside = swapped(own, "core")
+    state = call(attend_first, state_shapes, keys=2 * SRC_ROWS)(query_pair, own, own_beside)
+    early_across, *state = lax.optimization_barrier((early_across, *state))
+    early_both = swapped(early_across, "core")
+    state = call(attend_next, state_shapes, keys=2 * EARLY)(query_pair, early_across, early_both, *state)
+    late_across, *state = lax.optimization_barrier((late_across, *state))
+    late_both = swapped(late_across, "core")
+    state = call(attend_next, state_shapes, keys=SRC_ROWS - EARLY)(query_pair, late_across, *state)
+    message = call(
+        attend_last,
+        [((SLOTS, BACK, HD), BF16)],
+        [pltpu.VMEM((SRC_ROWS, HD), BF16)] * 2,
+        keys=SRC_ROWS - EARLY,
+    )(query_pair, late_both, *state)
     received = lax.all_to_all(message, ("yhi", "z"), 0, 0, tiled=True)
     attended, attended_t = call(unpack, [((LOCAL, D), BF16)] * 2, [pltpu.VMEM((16, D), BF16)], kept=False)(
         received

time: 106 us -> 103 us (0.972)
  local copies, waits for them, and re-layouts: 6.11 us -> 0 us
  starting transfers between devices: 5.75 us -> 9.85 us
  Pallas kernels: 13 us -> 11.3 us
    unnamed x16 -> x0, local copies, waits for them, and re-layouts: 6.11 us -> none
    ppermute x3 -> x5, starting transfers between devices: 5.75 us -> 9.85 us  [swapped(): return lax.ppermute(block, axis, [(0, 1), (1, 0)])]
    pallas_call x6 -> x7, Pallas kernels: 13 us -> 11.3 us  [run(): pl.pallas_call(kernel, out_shape=shapes[0] if one else shapes, in_specs=p...]
    ppermute x3 -> x5, waiting for transfers between devices: 13.3 us -> 14 us  [swapped(): return lax.ppermute(block, axis, [(0, 1), (1, 0)])]
  transfers between devices with their start and end apart: 3 -> 5, of which waited for: 1 -> 3; matrix products, arithmetic and copies ran while one was open for 0% -> 0% of each run, Pallas kernels for 4% -> 6%
where the time goes in v3:
time: 103 us; the launch traced here: 102 us
  blocking collectives  66.3 us (64%)
  waiting for transfers between devices  14 us (14%)
  Pallas kernels  11.3 us (11%)
  starting transfers between devices  9.85 us (10%)
    all_to_all x2, blocking collectives, local(): received = lax.all_to_all(message, ('yhi', 'z'), 0, 0, tiled=True)  66.3 us
    ppermute x5, waiting for transfers between devices, swapped(): return lax.ppermute(block, axis, [(0, 1), (1, 0)])  14 us
    pallas_call x7, Pallas kernels, run(): pl.pallas_call(kernel, out_shape=shapes[0] if one else shapes, in_specs=p...  11.3 us
    ppermute x5, starting transfers between devices, swapped(): return lax.ppermute(block, axis, [(0, 1), (1, 0)])  9.85 us
  transfers between devices with their start and end apart: 5, of which 3 were waited for; matrix products, arithmetic and copies ran while one was open for 0% of the time, Pallas kernels for 6%

profile of v3, /device:TPU:6, one launch (start us, length us, event | category | flops | bytes accessed | tf_op | source)
XLA Modules:
  0.0 102.3 jit_solution(1759334259456471410)
XLA Ops:
  0.6 2.4 %shard_map.95 = bf16[32,112,128]{2,1,0:T(8,128)(2,1)S(1)} custom-call(s32[1]{0:T(128)} %bitcast.first, bf16[18,3072]{1,0:T(8,128)(2,1)} %bitcast.11, bf16[18,3072]{1,0:T(8,128)(2,1)} %bitcast.12, bf16[18,3072]{1,0:T(8,128)(2,1)} %bitcast.13, bf16[18,3072]{1,0:T(8,128)(2,1)} %bitcast.14, bf16[18,3072]{1,0:T(8,128)(2,1)} %bitcast.15, ...), custom_call_target="tpu_custom_call" | custom-call | bytes 1000000 | tf_op jit(solution)/shard_map/pallas_call | solution.py:227
  3.1 43.8 %all_to_all.10.received = bf16[32,112,128]{2,1,0:T(8,128)(2,1)S(1)} all-to-all(bf16[32,112,128]{2,1,0:T(8,128)(2,1)S(1)} %shard_map.95), channel_id=1, replica_groups=mesh['yhi'=4,'core'=2,'z'=8,'ylo'=2,'x'=4] {'yhi','z'}, dimensions={0} | all-to-all | bytes 1835008 | tf_op jit(solution)/shard_map/all_to_all | solution.py:255
  46.9 0.5 shard_map.96
  47.4 1.9 %collective-permute-start.2 = (bf16[576,512]{1,0:T(8,128)(2,1)S(1)}, bf16[576,512]{1,0:T(8,128)(2,1)S(1)}, u32[]{:S(2)}, u32[]{:S(2)}) collective-permute-start(bf16[576,512]{1,0:T(8,128)(2,1)S(1)} %get-tuple-element.38.rest_0_), channel_id=1, source_target_pairs={{0,64},{64,0},{1,65},{65,1},{2,66},{66,2},{3,67},{67,3},{4,68},{68... | collective-permute-start | bytes 1769480 | tf_op jit(solution)/shard_map/ppermute | solution.py:263
  49.3 1.9 %collective-permute-start.1 = (bf16[320,512]{1,0:T(8,128)(2,1)S(1)}, bf16[320,512]{1,0:T(8,128)(2,1)S(1)}, u32[]{:S(2)}, u32[]{:S(2)}) collective-permute-start(bf16[320,512]{1,0:T(8,128)(2,1)S(1)} %get-tuple-element.37), channel_id=1, source_target_pairs={{0,4},{4,0},{1,5},{5,1},{2,6},{6,2},{3,7},{7,3},{8,12},{12,8},{9,1... | collective-permute-start | bytes 983048 | tf_op jit(solution)/shard_map/ppermute | solution.py:263
  51.3 0.0 collective-permute-done.2.rest_1_
  51.3 2.5 %shard_map.97 = (f32[576,1]{1,0:T(8,128)S(1)}, f32[576,1]{1,0:T(8,128)S(1)}, f32[576,1]{1,0:T(8,128)S(1)}, f32[576,128]{1,0:T(8,128)S(1)}, f32[576,128]{1,0:T(8,128)S(1)}) custom-call(bf16[576,256]{1,0:T(8,128)(2,1)S(1)} %get-tuple-element.35.query_pair, bf16[576,512]{1,0:T(8,128)(2,1)S(1)} %get-tuple-element.38.rest_0_, ...), custom_call_target="tpu_custom_call" | custom-call | flops 1358954496 | bytes 1000000 | tf_op jit(solution)/shard_map/pallas_call | solution.py:227
  53.8 7.6 %collective-permute-done.1.rest_0_ = bf16[320,512]{1,0:T(8,128)(2,1)S(1)} collective-permute-done((bf16[320,512]{1,0:T(8,128)(2,1)S(1)}, bf16[320,512]{1,0:T(8,128)(2,1)S(1)}, u32[]{:S(2)}, u32[]{:S(2)}) %collective-permute-start.1) | collective-permute-done | bytes 327712 | tf_op jit(solution)/shard_map/ppermute | solution.py:263
  61.3 1.9 %collective-permute-start.3 = (bf16[320,512]{1,0:T(8,128)(2,1)S(1)}, bf16[320,512]{1,0:T(8,128)(2,1)S(1)}, u32[]{:S(2)}, u32[]{:S(2)}) collective-permute-start(bf16[320,512]{1,0:T(8,128)(2,1)S(1)} %collective-permute-done.1.rest_0_), channel_id=1, source_target_pairs={{0,64},{64,0},{1,65},{65,1},{2,66},{66,2},{3,67},{67,3},{4,68},{68... | collective-permute-start | bytes 983048 | tf_op jit(solution)/shard_map/ppermute | solution.py:263
  63.2 2.2 %collective-permute-start = (bf16[256,512]{1,0:T(8,128)(2,1)S(1)}, bf16[256,512]{1,0:T(8,128)(2,1)S(1)}, u32[]{:S(2)}, u32[]{:S(2)}) collective-permute-start(bf16[256,512]{1,0:T(8,128)(2,1)S(1)} %get-tuple-element.36), channel_id=1, source_target_pairs={{0,4},{4,0},{1,5},{5,1},{2,6},{6,2},{3,7},{7,3},{8,12},{12,8},{9,1... | collective-permute-start | bytes 786440 | tf_op jit(solution)/shard_map/ppermute | solution.py:263
  65.5 0.0 collective-permute-done.3.rest_1_
  65.5 2.1 %shard_map.98 = (f32[576,1]{1,0:T(8,128)S(1)}, f32[576,1]{1,0:T(8,128)S(1)}, f32[576,1]{1,0:T(8,128)S(1)}, f32[576,128]{1,0:T(8,128)S(1)}, f32[576,128]{1,0:T(8,128)S(1)}) custom-call(bf16[576,256]{1,0:T(8,128)(2,1)S(1)} %get-tuple-element.35.query_pair, bf16[320,512]{1,0:T(8,128)(2,1)S(1)} %collective-permute-done.1.rest_0_, ...), custom_call_target="tpu_custom_call" | custom-call | flops 754974720 | bytes 1000000 | tf_op jit(solution)/shard_map/pallas_call | solution.py:227
  67.5 6.3 %collective-permute-done.rest_0_ = bf16[256,512]{1,0:T(8,128)(2,1)S(1)} collective-permute-done((bf16[256,512]{1,0:T(8,128)(2,1)S(1)}, bf16[256,512]{1,0:T(8,128)(2,1)S(1)}, u32[]{:S(2)}, u32[]{:S(2)}) %collective-permute-start) | collective-permute-done | bytes 262176 | tf_op jit(solution)/shard_map/ppermute | solution.py:263
  73.9 1.9 %collective-permute-start.4 = (bf16[256,512]{1,0:T(8,128)(2,1)S(1)}, bf16[256,512]{1,0:T(8,128)(2,1)S(1)}, u32[]{:S(2)}, u32[]{:S(2)}) collective-permute-start(bf16[256,512]{1,0:T(8,128)(2,1)S(1)} %collective-permute-done.rest_0_), channel_id=1, source_target_pairs={{0,64},{64,0},{1,65},{65,1},{2,66},{66,2},{3,67},{67,3},{4,68},{68... | collective-permute-start | bytes 786440 | tf_op jit(solution)/shard_map/ppermute | solution.py:263
  75.8 1.4 %shard_map.99 = (f32[576,1]{1,0:T(8,128)S(1)}, f32[576,1]{1,0:T(8,128)S(1)}, f32[576,1]{1,0:T(8,128)S(1)}, f32[576,128]{1,0:T(8,128)S(1)}, f32[576,128]{1,0:T(8,128)S(1)}) custom-call(bf16[576,256]{1,0:T(8,128)(2,1)S(1)} %get-tuple-element.35.query_pair, bf16[256,512]{1,0:T(8,128)(2,1)S(1)} %collective-permute-done.rest_0_, ...), custom_call_target="tpu_custom_call" | custom-call | flops 301989888 | bytes 1000000 | tf_op jit(solution)/shard_map/pallas_call | solution.py:227
  77.1 0.1 collective-permute-done.4.kv
  77.3 1.6 %shard_map.100 = bf16[32,40,128]{2,1,0:T(8,128)(2,1)S(1)} custom-call(bf16[576,256]{1,0:T(8,128)(2,1)S(1)} %get-tuple-element.35.query_pair, bf16[256,512]{1,0:T(8,128)(2,1)S(1)} %collective-permute-done.4.kv, f32[576,1]{1,0:T(8,128)S(1)} %get-tuple-element.61.rest_0_, f32[576,1]{1,0:T(8,128)S(1)} %get-tuple-element.62.rest_1_, ...), custom_call_target="tpu_custom_call" | custom-call | flops 301989888 | bytes 1000000 | tf_op jit(solution)/shard_map/pallas_call | solution.py:227
  78.9 22.5 %all_to_all.11.received = bf16[32,40,128]{2,1,0:T(8,128)(2,1)S(1)} all-to-all(bf16[32,40,128]{2,1,0:T(8,128)(2,1)S(1)} %shard_map.100), channel_id=1, replica_groups=mesh['yhi'=4,'core'=2,'z'=8,'ylo'=2,'x'=4] {'yhi','z'}, dimensions={0} | all-to-all | bytes 655360 | tf_op jit(solution)/shard_map/all_to_all | solution.py:281
  101.4 0.9 shard_map.101
Async XLA Ops:
  47.4 3.9 %collective-permute-start.2 = (bf16[576,512]{1,0:T(8,128)(2,1)S(1)}, bf16[576,512]{1,0:T(8,128)(2,1)S(1)}, u32[]{:S(2)}, u32[]{:S(2)}) collective-permute-start(bf16[576,512]{1,0:T(8,128)(2,1)S(1)} %get-tuple-element.38.rest_0_), channel_id=1, source_target_pairs={{0,64},{64,0},{1,65},{65,1},{2,66},{66,2},{3,67},{67,3},{4,68},{68... | collective-permute-start | bytes 1769480 | tf_op jit(solution)/shard_map/ppermute | solution.py:263
  49.3 12.0 %collective-permute-start.1 = (bf16[320,512]{1,0:T(8,128)(2,1)S(1)}, bf16[320,512]{1,0:T(8,128)(2,1)S(1)}, u32[]{:S(2)}, u32[]{:S(2)}) collective-permute-start(bf16[320,512]{1,0:T(8,128)(2,1)S(1)} %get-tuple-element.37), channel_id=1, source_target_pairs={{0,4},{4,0},{1,5},{5,1},{2,6},{6,2},{3,7},{7,3},{8,12},{12,8},{9,1... | collective-permute-start | bytes 983048 | tf_op jit(solution)/shard_map/ppermute | solution.py:263
  61.3 4.1 %collective-permute-start.3 = (bf16[320,512]{1,0:T(8,128)(2,1)S(1)}, bf16[320,512]{1,0:T(8,128)(2,1)S(1)}, u32[]{:S(2)}, u32[]{:S(2)}) collective-permute-start(bf16[320,512]{1,0:T(8,128)(2,1)S(1)} %collective-permute-done.1.rest_0_), channel_id=1, source_target_pairs={{0,64},{64,0},{1,65},{65,1},{2,66},{66,2},{3,67},{67,3},{4,68},{68... | collective-permute-start | bytes 983048 | tf_op jit(solution)/shard_map/ppermute | solution.py:263
  63.2 10.6 %collective-permute-start = (bf16[256,512]{1,0:T(8,128)(2,1)S(1)}, bf16[256,512]{1,0:T(8,128)(2,1)S(1)}, u32[]{:S(2)}, u32[]{:S(2)}) collective-permute-start(bf16[256,512]{1,0:T(8,128)(2,1)S(1)} %get-tuple-element.36), channel_id=1, source_target_pairs={{0,4},{4,0},{1,5},{5,1},{2,6},{6,2},{3,7},{7,3},{8,12},{12,8},{9,1... | collective-permute-start | bytes 786440 | tf_op jit(solution)/shard_map/ppermute | solution.py:263
  73.9 3.4 %collective-permute-start.4 = (bf16[256,512]{1,0:T(8,128)(2,1)S(1)}, bf16[256,512]{1,0:T(8,128)(2,1)S(1)}, u32[]{:S(2)}, u32[]{:S(2)}) collective-permute-start(bf16[256,512]{1,0:T(8,128)(2,1)S(1)} %collective-permute-done.rest_0_), channel_id=1, source_target_pairs={{0,64},{64,0},{1,65},{65,1},{2,66},{66,2},{3,67},{67,3},{4,68},{68... | collective-permute-start | bytes 786440 | tf_op jit(solution)/shard_map/ppermute | solution.py:263

commit v4 on v3

--- a/solution.py
+++ b/solution.py
@@ -16,11 +16,12 @@
 ROWS = 144
 LOCAL = 18
 MAIN = 16
-SLOTS = 32
-SRC_ROWS = 576
-EARLY = 320
-SEND = 112
-BACK = 40
+CHIPS = 64
+KEYS = 1152
+QUERIES = 576
+HALF = 9
+SEND = 96
+BACK = 24
 EPSILON = 1e-06
 THETA = 10000.0
 SCALE = 1.0 / math.sqrt(HD)
@@ -32,8 +33,8 @@
 HBM = pl.BlockSpec(memory_space=pltpu.HBM)
 
 
-def slot_of(head):
-    return (head % 3) * 8 + head // 3
+def chip_of(head, half):
+    return (head % 3) * 16 + head // 3 * 2 + half
 
 
 def lanes(head):
@@ -88,47 +89,64 @@
         return (x_turned * inverse).astype(BF16), dotted.astype(BF16)
 
     tails[...] = jnp.zeros_like(tails)
-    for slot in range(HEADS, SLOTS):
-        out[slot] = jnp.zeros((SEND, HD), BF16)
+    for chip in range(2 * HEADS, CHIPS):
+        out[chip] = jnp.zeros((SEND, HD), BF16)
     for copy in copies:
         copy.wait()
     of_query = turned(query_gain[...])
     of_key = turned(key_gain[...])
     for head in range(HEADS):
         here = lanes(head)
-        slot = slot_of(head)
         q_hat, q_dot = normalize(query[:, here], query_t[:, here], *of_query)
         k_hat, k_dot = normalize(key[:, here], key_t[:, here], *of_key)
-        parts = (q_hat, q_dot, k_hat, k_dot, value[:, here], value_t[:, here])
-        for t, part in enumerate(parts):
-            out[slot, 16 * t : 16 * t + 16, :] = part[:MAIN]
-            tails[16 * t : 16 * t + 2, here] = part[MAIN:]
-    pick = one_hot((16, 96), lambda r: (r >> 1) * 16 + (r & 1), lambda r: r < 12)
+        tails[0:LOCAL, here] = q_hat
+        tails[32 : 32 + LOCAL, here] = q_dot
+        for t, part in enumerate((k_hat, k_dot, value[:, here], value_t[:, here])):
+            for half in range(2):
+                out[chip_of(head, half), 16 * t : 16 * t + 16, :] = part[:MAIN]
+            tails[64 + 16 * t : 66 + 16 * t, here] = part[MAIN:]
+
+    def column(r):
+        half = r >> 5
+        r = r & 31
+        from_query = jnp.where(r < 8 + HALF, r - 8, r - 8 - HALF + 32) + HALF * half
+        return jnp.where(r < 8, 64 + 16 * (r >> 1) + (r & 1), from_query)
+
+    pick = one_hot((64, 128), column, lambda r: (r & 31) < 8 + 2 * HALF)
     slab = jnp.dot(pick, tails[...], preferred_element_type=F32).astype(BF16)
     for head in range(HEADS):
-        out[slot_of(head), 96:112, :] = slab[:, lanes(head)]
-
-
-def repack(received, query_pair, own, early, late):
-    for source in range(SLOTS):
+        for half in range(2):
+            out[chip_of(head, half), 64:96, :] = slab[32 * half : 32 * half + 32, lanes(head)]
+
+
+def repack(received, query_pair, own):
+    for source in range(CHIPS):
         row = 16 * source
-        key_value, row_there = (early, row) if row < EARLY else (late, row - EARLY)
-        for t, at in enumerate((128, 0, 0, 128, 256, 384)):
-            part = received[source, 16 * t : 16 * t + 16, :]
-            if t < 2:
-                query_pair[row : row + 16, at : at + HD] = part
-            else:
-                own[row : row + 16, at : at + HD] = part
-                key_value[row_there : row_there + 16, at : at + HD] = part
-    slabs = received[:, 96:112, :].reshape(SLOTS * 16, HD)
-    for t, at in enumerate((128, 0, 0, 128, 256, 384)):
-        pick = one_hot((64, 512), lambda r: (r >> 1) * 16 + 2 * t + (r & 1), lambda r: r >= 0)
-        part = jnp.dot(pick, slabs, preferred_element_type=F32).astype(BF16)
-        if t < 2:
-            query_pair[512:576, at : at + HD] = part
-        else:
-            own[512:576, at : at + HD] = part
-            late[512 - EARLY : 576 - EARLY, at : at + HD] = part
+        for t in range(4):
+            own[row : row + 16, HD * t : HD * t + HD] = received[source, 16 * t : 16 * t + 16, :]
+
+    def column(r):
+        query = r // HALF
+        dotted = query >= 16
+        from_query = (query & 15) * 32 + 8 + jnp.where(dotted, HALF, 0) + (r - query * HALF)
+        rest = r - 288
+        from_rest = ((rest & 31) >> 1) * 32 + (rest >> 5) * 2 + (rest & 1)
+        return jnp.where(r < 288, from_query, from_rest)
+
+    pick = one_hot((416, 512), column, lambda r: r >= 0)
+    for two in range(2):
+        slabs = [
+            received[32 * two + 16 * g : 32 * two + 16 * g + 16, 64:96, :].reshape(512, HD) for g in range(2)
+        ]
+        picked = jnp.dot(pick, jnp.concatenate(slabs, axis=1), preferred_element_type=F32).astype(BF16)
+        for g in range(2):
+            group = 2 * two + g
+            here = lanes(g)
+            query_pair[144 * group : 144 * group + 144, HD:] = picked[0:144, here]
+            query_pair[144 * group : 144 * group + 144, :HD] = picked[144:288, here]
+            for t in range(4):
+                rows = slice(1024 + 32 * group, 1024 + 32 * group + 32)
+                own[rows, HD * t : HD * t + HD] = picked[288 + 32 * t : 320 + 32 * t, here]
 
 
 TRANSPOSED = (((1,), (1,)), ((), ()))
@@ -161,20 +179,13 @@
     return peak, old[0] + total, old[1] + drift, old[2] + summed, old[3] + summed_dot
 
 
-QUERY_BLOCKS = [slice(b, b + BQ) for b in range(0, SRC_ROWS, BQ)]
+QUERY_BLOCKS = [slice(b, b + BQ) for b in range(0, QUERIES, BQ)]
 
 
 def attend_first(query_pair, *rest):
     blocks, state = rest[:-5], rest[-5:]
     for at in QUERY_BLOCKS:
         for ref, part in zip(state, absorb(query_pair, blocks, at, None)):
-            ref[at, :] = part
-
-
-def attend_next(query_pair, *rest):
-    blocks, before, after = rest[:-10], rest[-10:-5], rest[-5:]
-    for at in QUERY_BLOCKS:
-        for ref, part in zip(after, absorb(query_pair, blocks, at, [ref[at, :] for ref in before])):
             ref[at, :] = part
 
 
@@ -185,32 +196,39 @@
         _, total, drift, summed, summed_dot = state
         attended[at, :] = (summed / total).astype(BF16)
         attended_t[at, :] = ((summed_dot - drift / total * summed) / total).astype(BF16)
-    for source in range(SLOTS):
-        at = slice(16 * source, 16 * source + 16)
-        out[source, 0:16, :] = attended[at, :]
-        out[source, 16:32, :] = attended_t[at, :]
-    tail = jnp.concatenate([attended[512:576, :], attended_t[512:576, :]], axis=0)
-    pick = one_hot(
-        (256, 128),
-        lambda r: (r >> 3) * 2 + (r & 1) + jnp.where((r & 2) > 0, 64, 0),
-        lambda r: (r & 7) < 4,
-    )
-    slabs = jnp.dot(pick, tail, preferred_element_type=F32).astype(BF16)
-    out[:, 32:40, :] = slabs.reshape(SLOTS, 8, HD)
-
-
-def unpack(received, attended, attended_t, tails):
-    tails[...] = jnp.zeros_like(tails)
+
+    def column(r):
+        source = r // BACK
+        r = r - source * BACK
+        return source * HALF + jnp.where(r < HALF, r, r - HALF + 144)
+
+    pick = one_hot((16 * BACK, 288), column, lambda r: r % BACK < 2 * HALF)
+    for two in range(2):
+        sides = []
+        for group in (2 * two, 2 * two + 1):
+            at = slice(144 * group, 144 * group + 144)
+            sides.append(jnp.concatenate([attended[at, :], attended_t[at, :]], axis=0))
+        picked = jnp.dot(pick, jnp.concatenate(sides, axis=1), preferred_element_type=F32).astype(BF16)
+        for g in range(2):
+            sources = slice(16 * (2 * two + g), 16 * (2 * two + g) + 16)
+            out[sources, :, :] = picked[:, lanes(g)].reshape(16, BACK, HD)
+
+
+def unpack(received, attended, attended_t, both):
+    both[...] = jnp.zeros_like(both)
     for head in range(HEADS):
-        slot = slot_of(head)
-        here = lanes(head)
-        attended[0:16, here] = received[slot, 0:16, :]
-        attended_t[0:16, here] = received[slot, 16:32, :]
-        tails[0:8, here] = received[slot, 32:40, :]
-    pick = one_hot((16, 16), lambda r: jnp.where(r < 8, r, r - 6), lambda r: (r & 7) < 2)
-    rest = jnp.dot(pick, tails[...], preferred_element_type=F32)
-    attended[16:18, :] = rest[0:2].astype(BF16)
-    attended_t[16:18, :] = rest[8:10].astype(BF16)
+        for half in range(2):
+            both[32 * half : 32 * half + BACK, lanes(head)] = received[chip_of(head, half)]
+
+    def from_message(r):
+        row = r & 31
+        half = jnp.where(row >= HALF, 1, 0)
+        return 32 * half + row - HALF * half + jnp.where(r >= 32, HALF, 0)
+
+    pick = one_hot((64, 64), from_message, lambda r: (r & 31) < LOCAL)
+    rows = jnp.dot(pick, both[...], preferred_element_type=F32)
+    attended[...] = rows[0:LOCAL].astype(BF16)
+    attended_t[...] = rows[32 : 32 + LOCAL].astype(BF16)
 
 
 def call(kernel, outs, scratch=(), specs=None, kept=True, keys=0):
@@ -231,9 +249,10 @@
             out_specs=VMEM if one else (VMEM,) * len(shapes),
             scratch_shapes=list(scratch),
             cost_estimate=pl.CostEstimate(
-                flops=16 * SRC_ROWS * HD * keys, transcendentals=SRC_ROWS * keys, bytes_accessed=10**6
+                flops=16 * QUERIES * HD * keys, transcendentals=QUERIES * keys, bytes_accessed=10**6
             ),
             compiler_params=pltpu.CompilerParams(vmem_limit_bytes=24 * 2**20),
+            name=kernel.__name__,
         )(*args)
 
     return run
@@ -248,38 +267,20 @@
     landing.append(pltpu.SemaphoreType.DMA((8,)))
     message = call(
         prepare,
-        [((SLOTS, SEND, HD), BF16)],
-        [pltpu.VMEM((96, D), BF16)] + landing,
+        [((CHIPS, SEND, HD), BF16)],
+        [pltpu.VMEM((128, D), BF16)] + landing,
         specs=[SMEM] + [HBM] * 8,
     )(first, *rows, query_gain.reshape(1, HD), key_gain.reshape(1, HD))
-    received = lax.all_to_all(message, ("yhi", "z"), 0, 0, tiled=True)
-    query_pair, own, early, late = call(
-        repack,
-        [((SRC_ROWS, 2 * HD), BF16)] + [((n, 4 * HD), BF16) for n in (SRC_ROWS, EARLY, SRC_ROWS - EARLY)],
-    )(received)
-    state_shapes = [((SRC_ROWS, 1), F32)] * 3 + [((SRC_ROWS, HD), F32)] * 2
-
-    def swapped(block, axis):
-        return lax.ppermute(block, axis, [(0, 1), (1, 0)])
-
-    early_across = swapped(early, "ylo")
-    late_across = swapped(late, "ylo")
-    own_beside = swapped(own, "core")
-    state = call(attend_first, state_shapes, keys=2 * SRC_ROWS)(query_pair, own, own_beside)
-    early_across, *state = lax.optimization_barrier((early_across, *state))
-    early_both = swapped(early_across, "core")
-    state = call(attend_next, state_shapes, keys=2 * EARLY)(query_pair, early_across, early_both, *state)
-    late_across, *state = lax.optimization_barrier((late_across, *state))
-    late_both = swapped(late_across, "core")
-    state = call(attend_next, state_shapes, keys=SRC_ROWS - EARLY)(query_pair, late_across, *state)
+    received = lax.all_to_all(message, ("yhi", "z", "ylo"), 0, 0, tiled=True)
+    query_pair, own = call(repack, [((QUERIES, 2 * HD), BF16), ((KEYS, 4 * HD), BF16)])(received)
+    beside = lax.ppermute(own, "core", [(0, 1), (1, 0)])
+    state_shapes = [((QUERIES, 1), F32)] * 3 + [((QUERIES, HD), F32)] * 2
+    state = call(attend_first, state_shapes, keys=KEYS)(query_pair, own)
     message = call(
-        attend_last,
-        [((SLOTS, BACK, HD), BF16)],
-        [pltpu.VMEM((SRC_ROWS, HD), BF16)] * 2,
-        keys=SRC_ROWS - EARLY,
-    )(query_pair, late_both, *state)
-    received = lax.all_to_all(message, ("yhi", "z"), 0, 0, tiled=True)
-    attended, attended_t = call(unpack, [((LOCAL, D), BF16)] * 2, [pltpu.VMEM((16, D), BF16)], kept=False)(
+        attend_last, [((CHIPS, BACK, HD), BF16)], [pltpu.VMEM((QUERIES, HD), BF16)] * 2, keys=KEYS
+    )(query_pair, beside, *state)
+    received = lax.all_to_all(message, ("yhi", "z", "ylo"), 0, 0, tiled=True)
+    attended, attended_t = call(unpack, [((LOCAL, D), BF16)] * 2, [pltpu.VMEM((64, D), BF16)], kept=False)(
         received
     )
     return attended.reshape(1, LOCAL, D), attended_t.reshape(1, LOCAL, D)

time: 103 us -> 92.5 us (0.90)
  blocking collectives: 66.3 us -> 79.8 us
  waiting for transfers between devices: 14 us -> 0.51 us
  starting transfers between devices: 9.85 us -> 1.92 us
  Pallas kernels: 11.3 us -> 9.36 us
    ppermute x5 -> x1, waiting for transfers between devices: 14 us -> 0.51 us  [local(): beside = lax.ppermute(own, 'core', [(0, 1), (1, 0)])]
    all_to_all x2, blocking collectives: 66.3 us -> 79.8 us  [local(): received = lax.all_to_all(message, ('yhi', 'z', 'ylo'), 0, 0, tiled=True)]
    ppermute x5 -> x1, starting transfers between devices: 9.85 us -> 1.92 us  [local(): beside = lax.ppermute(own, 'core', [(0, 1), (1, 0)])]
    pallas_call x7 -> x5, Pallas kernels: 11.3 us -> 9.36 us  [run(): pl.pallas_call(kernel, out_shape=shapes[0] if one else shapes, in_specs=p...]
  transfers between devices with their start and end apart: 5 -> 1, of which waited for: 3 -> 1; matrix products, arithmetic and copies ran while one was open for 0% -> 0% of each run, Pallas kernels for 6% -> 2%
where the time goes in v4:
time: 92.5 us; the launch traced here: 92.3 us
  blocking collectives  79.8 us (86%)
  Pallas kernels  9.36 us (10%)
  starting transfers between devices  1.92 us (2%)
    all_to_all x2, blocking collectives, local(): received = lax.all_to_all(message, ('yhi', 'z', 'ylo'), 0, 0, tiled=True)  79.8 us
    pallas_call x5, Pallas kernels, run(): pl.pallas_call(kernel, out_shape=shapes[0] if one else shapes, in_specs=p...  9.36 us
    ppermute x1, starting transfers between devices, local(): beside = lax.ppermute(own, 'core', [(0, 1), (1, 0)])  1.92 us
  transfers between devices with their start and end apart: 1, of which 1 were waited for; matrix products, arithmetic and copies ran while one was open for 0% of the time, Pallas kernels for 2%

profile of v4, /device:TPU:6, one launch (start us, length us, event | category | flops | bytes accessed | tf_op | source)
XLA Modules:
  0.0 92.3 jit_solution(7790724738745337768)
XLA Ops:
  0.6 2.5 %prepare.1 = bf16[64,96,128]{2,1,0:T(8,128)(2,1)S(1)} custom-call(s32[1]{0:T(128)} %bitcast.first, bf16[18,3072]{1,0:T(8,128)(2,1)} %bitcast.11, bf16[18,3072]{1,0:T(8,128)(2,1)} %bitcast.12, bf16[18,3072]{1,0:T(8,128)(2,1)} %bitcast.13, bf16[18,3072]{1,0:T(8,128)(2,1)} %bitcast.14, bf16[18,3072]{1,0:T(8,128)(2,1)} %bitcast.15, bf16[18,3072]{1,0:T(8,128)(2,1)} %bitcast.16, ...), custom_call_target="tpu_custom_call" | custom-call | bytes 1000000 | tf_op jit(solution)/shard_map/prepare/pallas_call | solution.py:245
  3.1 56.0 %all_to_all.10.received = bf16[64,96,128]{2,1,0:T(8,128)(2,1)S(1)} all-to-all(bf16[64,96,128]{2,1,0:T(8,128)(2,1)S(1)} %prepare.1), channel_id=1, replica_groups=mesh['yhi'=4,'core'=2,'z'=8,'ylo'=2,'x'=4] {'yhi','z','ylo'}, dimensions={0} | all-to-all | bytes 3145728 | tf_op jit(solution)/shard_map/all_to_all | solution.py:274
  59.1 0.5 repack.1
  59.6 1.9 %collective-permute-start = (bf16[1152,512]{1,0:T(8,128)(2,1)S(1)}, bf16[1152,512]{1,0:T(8,128)(2,1)S(1)}, u32[]{:S(2)}, u32[]{:S(2)}) collective-permute-start(bf16[1152,512]{1,0:T(8,128)(2,1)S(1)} %get-tuple-element.12.rest_0_), channel_id=1, source_target_pairs={{0,64},{64,0},{1,65},{65,1},{2,66},{66,2},{3,67},{67,3},{4,68},{68... | collective-permute-start | bytes 3538952 | tf_op jit(solution)/shard_map/ppermute | solution.py:276
  61.6 2.3 %attend_first.1 = (f32[576,1]{1,0:T(8,128)S(1)}, f32[576,1]{1,0:T(8,128)S(1)}, f32[576,1]{1,0:T(8,128)S(1)}, f32[576,128]{1,0:T(8,128)S(1)}, f32[576,128]{1,0:T(8,128)S(1)}) custom-call(bf16[576,256]{1,0:T(8,128)(2,1)S(1)} %get-tuple-element.11.query_pair, bf16[1152,512]{1,0:T(8,128)(2,1)S(1)} %get-tuple-element.12.rest_0_), custom_call_target="tpu_custom_call" | custom-call | flops 1358954496 | bytes 1000000 | tf_op jit(solution)/shard_map/attend_first/pallas_call | solution.py:245
  63.9 0.5 collective-permute-done.kv
  64.4 3.0 %attend_last.1 = bf16[64,24,128]{2,1,0:T(8,128)(2,1)S(1)} custom-call(bf16[576,256]{1,0:T(8,128)(2,1)S(1)} %get-tuple-element.11.query_pair, bf16[1152,512]{1,0:T(8,128)(2,1)S(1)} %collective-permute-done.kv, f32[576,1]{1,0:T(8,128)S(1)} %get-tuple-element.13.rest_0_, f32[576,1]{1,0:T(8,128)S(1)} %get-tuple-element.14.rest_1_, ...), custom_call_target="tpu_custom_call" | custom-call | flops 1358954496 | bytes 1000000 | tf_op jit(solution)/shard_map/attend_last/pallas_call | solution.py:245
  67.4 23.8 %all_to_all.11.received = bf16[64,24,128]{2,1,0:T(8,128)(2,1)S(1)} all-to-all(bf16[64,24,128]{2,1,0:T(8,128)(2,1)S(1)} %attend_last.1), channel_id=1, replica_groups=mesh['yhi'=4,'core'=2,'z'=8,'ylo'=2,'x'=4] {'yhi','z','ylo'}, dimensions={0} | all-to-all | bytes 786432 | tf_op jit(solution)/shard_map/all_to_all | solution.py:282
  91.3 1.0 %unpack.1 = (bf16[18,3072]{1,0:T(8,128)(2,1)}, bf16[18,3072]{1,0:T(8,128)(2,1)}) custom-call(bf16[64,24,128]{2,1,0:T(8,128)(2,1)S(1)} %all_to_all.11.received), custom_call_target="tpu_custom_call" | custom-call | bytes 1000000 | tf_op jit(solution)/shard_map/unpack/pallas_call | solution.py:245
Async XLA Ops:
  59.6 4.7 %collective-permute-start = (bf16[1152,512]{1,0:T(8,128)(2,1)S(1)}, bf16[1152,512]{1,0:T(8,128)(2,1)S(1)}, u32[]{:S(2)}, u32[]{:S(2)}) collective-permute-start(bf16[1152,512]{1,0:T(8,128)(2,1)S(1)} %get-tuple-element.12.rest_0_), channel_id=1, source_target_pairs={{0,64},{64,0},{1,65},{65,1},{2,66},{66,2},{3,67},{67,3},{4,68},{68... | collective-permute-start | bytes 3538952 | tf_op jit(solution)/shard_map/ppermute | solution.py:276

commit v5 on v4

v5 whole, which is shorter than its diff:
```python
import math

import jax
import jax.numpy as jnp
from jax import lax
from jax.experimental import pallas as pl
from jax.experimental.pallas import tpu as pltpu
from jax.sharding import Mesh
from jax.sharding import PartitionSpec as P

HEADS = 24
HD = 128
D = 3072
TXT = 512
GRID_W = 64
ROWS = 144
LOCAL = 18
CHIPS = 64
KEYS = 1152
QUERIES = 576
HALF = 9
SEND = 90
BACK = 18
EPSILON = 1e-06
THETA = 10000.0
SCALE = 1.0 / math.sqrt(HD)
F32 = jnp.float32
BF16 = jnp.bfloat16

VMEM = pl.BlockSpec(memory_space=pltpu.VMEM)
SMEM = pl.BlockSpec(memory_space=pltpu.SMEM)
HBM = pl.BlockSpec(memory_space=pltpu.HBM)


def chip_of(head, half):
    return (head % 3) * 16 + head // 3 * 2 + half


def lanes(head):
    return slice(head * HD, (head + 1) * HD)


def prepare(first, *refs):
    sources, out, buffers, arrival = refs[:8], refs[8], refs[9:17], refs[17]
    copies = [
        pltpu.make_async_copy(source, buffer, arrival.at[i])
        for i, (source, buffer) in enumerate(zip(sources, buffers))
    ]
    for copy in copies:
        copy.start()
    query, key, value, query_t, key_t, value_t, query_gain, key_gain = buffers
    token = first[0] + lax.broadcasted_iota(jnp.int32, (LOCAL, HD), 0)
    lane = lax.broadcasted_iota(jnp.int32, (LOCAL, HD), 1)
    patch = jnp.maximum(token - TXT, 0)
    is_image = token >= TXT
    row_id = jnp.where(is_image, lax.shift_right_logical(patch, 6), 0).astype(F32)
    column_id = jnp.where(is_image, patch & (GRID_W - 1), 0).astype(F32)
    pair = lax.shift_right_logical(lane, 1)
    of_row = pair < 36
    step = jnp.where(of_row, pair - 8, pair - 36).astype(F32)
    frequency = jnp.exp(-math.log(THETA) * (step * (2.0 / 56.0)))
    angle = jnp.where(pair < 8, 0.0, jnp.where(of_row, row_id, column_id) * frequency)
    cosine = jnp.cos(angle)
    even = (lane & 1) == 0
    sine = jnp.where(even, -jnp.sin(angle), jnp.sin(angle))

    def turned(gain):
        wide = jnp.broadcast_to(gain, (LOCAL, HD))
        partner = jnp.where(even, pltpu.roll(wide, HD - 1, 1), pltpu.roll(wide, 1, 1))
        return wide * cosine, partner * sine

    row = lax.broadcasted_iota(jnp.int32, (HD, HD), 0)
    column = lax.broadcasted_iota(jnp.int32, (HD, HD), 1)
    exchange = jnp.where((row ^ 1) == column, 1.0, 0.0).astype(BF16)

    def normalize(raw, tangent, own, other):
        x = raw.astype(F32)
        u = tangent.astype(F32)
        inverse = lax.rsqrt(jnp.mean(x * x, axis=1, keepdims=True) + EPSILON)
        coupling = jnp.mean(x * u, axis=1, keepdims=True)
        x_turned = x * own + jnp.dot(raw, exchange, preferred_element_type=F32) * other
        u_turned = u * own + jnp.dot(tangent, exchange, preferred_element_type=F32) * other
        dotted = u_turned * inverse - x_turned * (inverse * inverse * inverse * coupling)
        return x_turned * inverse, dotted

    idle = 2 * HEADS * SEND
    out[idle:, :] = jnp.zeros((CHIPS * SEND - idle, HD), BF16)
    for copy in copies:
        copy.wait()
    of_query = turned(query_gain[...])
    of_key = turned(key_gain[...])
    for head in range(HEADS):
        here = lanes(head)
        q_hat, q_dot = normalize(query[:, here], query_t[:, here], *of_query)
        k_hat, k_dot = normalize(key[:, here], key_t[:, here], *of_key)
        parts = (k_hat.astype(BF16), k_dot.astype(BF16), value[:, here], value_t[:, here])
        for half in range(2):
            at = chip_of(head, half) * SEND
            for t, part in enumerate(parts):
                out[at + LOCAL * t : at + LOCAL * t + LOCAL, :] = part
            ours = slice(HALF * half, HALF * half + HALF)
            queries = jnp.concatenate([q_hat[ours], q_dot[ours]], axis=0)
            out[at + 4 * LOCAL : at + SEND, :] = queries.astype(BF16)


def repack(received, query_pair, own):
    for source in range(CHIPS):
        at = source * SEND
        for t in range(4):
            own[LOCAL * source : LOCAL * source + LOCAL, HD * t : HD * t + HD] = received[
                at + LOCAL * t : at + LOCAL * t + LOCAL, :
            ]
    for source in range(0, CHIPS, 2):
        two = [received[s * SEND + 4 * LOCAL : s * SEND + SEND, :].astype(F32) for s in (source, source + 1)]
        rows = slice(HALF * source, HALF * source + LOCAL)
        query_pair[rows, HD:] = jnp.concatenate([part[:HALF] for part in two], axis=0).astype(BF16)
        query_pair[rows, :HD] = jnp.concatenate([part[HALF:] for part in two], axis=0).astype(BF16)


TRANSPOSED = (((1,), (1,)), ((), ()))
BQ = 192


def absorb(query_pair, blocks, at, state):
    pair = query_pair[at, :]
    hat = query_pair[at, HD:]
    scores = [lax.dot_general(hat, kv[:, 0:HD], TRANSPOSED, preferred_element_type=F32) for kv in blocks]
    peak = None if state is None else state[0]
    for s in scores:
        top = jnp.max(s, axis=1, keepdims=True)
        peak = top if peak is None else jnp.maximum(peak, top)
    total = drift = both = extra = 0.0
    for s, kv in zip(scores, blocks):
        weights = jnp.exp2((s - peak) * (SCALE * math.log2(math.e)))
        moved = lax.dot_general(pair, kv[:, 0 : 2 * HD], TRANSPOSED, preferred_element_type=F32)
        product = weights * (moved * SCALE)
        total = total + jnp.sum(weights, axis=1, keepdims=True)
        drift = drift + jnp.sum(product, axis=1, keepdims=True)
        both = both + jnp.dot(weights.astype(BF16), kv[:, 2 * HD : 4 * HD], preferred_element_type=F32)
        extra = extra + jnp.dot(product.astype(BF16), kv[:, 2 * HD : 3 * HD], preferred_element_type=F32)
    summed = both[:, :HD]
    summed_dot = both[:, HD:] + extra
    if state is None:
        return peak, total, drift, summed, summed_dot
    rescale = jnp.exp2((state[0] - peak) * (SCALE * math.log2(math.e)))
    old = [part * rescale for part in state[1:]]
    return peak, old[0] + total, old[1] + drift, old[2] + summed, old[3] + summed_dot


QUERY_BLOCKS = [slice(b, b + BQ) for b in range(0, QUERIES, BQ)]


def attend_first(query_pair, *rest):
    blocks, state = rest[:-5], rest[-5:]
    for at in QUERY_BLOCKS:
        for ref, part in zip(state, absorb(query_pair, blocks, at, None)):
            ref[at, :] = part


def attend_last(query_pair, kv, *rest):
    before, (out, attended, attended_t) = rest[:5], rest[5:]
    for at in QUERY_BLOCKS:
        state = absorb(query_pair, (kv,), at, [ref[at, :] for ref in before])
        _, total, drift, summed, summed_dot = state
        attended[at, :] = summed / total
        attended_t[at, :] = (summed_dot - drift / total * summed) / total
    for source in range(CHIPS):
        rows = slice(HALF * source, HALF * source + HALF)
        both = jnp.concatenate([attended[rows, :], attended_t[rows, :]], axis=0)
        out[BACK * source : BACK * source + BACK, :] = both.astype(BF16)


def unpack(received, attended, attended_t):
    for head in range(HEADS):
        halves = []
        for half in range(2):
            at = chip_of(head, half) * BACK
            halves.append(received[at : at + BACK, :].astype(F32))
        here = lanes(head)
        attended[:, here] = jnp.concatenate([part[:HALF] for part in halves], axis=0).astype(BF16)
        attended_t[:, here] = jnp.concatenate([part[HALF:] for part in halves], axis=0).astype(BF16)


def call(kernel, outs, scratch=(), specs=None, kept=True, keys=0):
    make = pltpu.VMEM if kept else jax.ShapeDtypeStruct
    shapes = tuple(make(shape, dtype) for shape, dtype in outs)
    one = len(shapes) == 1

    def run(*args):
        places = specs or [VMEM] * len(args)
        args = [
            a if spec is SMEM else pltpu.with_memory_space_constraint(a, spec.memory_space)
            for a, spec in zip(args, places)
        ]
        return pl.pallas_call(
            kernel,
            out_shape=shapes[0] if one else shapes,
            in_specs=places,
            out_specs=VMEM if one else (VMEM,) * len(shapes),
            scratch_shapes=list(scratch),
            cost_estimate=pl.CostEstimate(
                flops=16 * QUERIES * HD * keys, transcendentals=QUERIES * keys, bytes_accessed=10**6
            ),
            compiler_params=pltpu.CompilerParams(vmem_limit_bytes=24 * 2**20),
            name=kernel.__name__,
        )(*args)

    return run


def exchanged(message, rows):
    pairs = message.reshape(CHIPS, rows // 2, 2, HD)
    pairs = lax.all_to_all(pairs, ("yhi", "z", "ylo"), 0, 0, tiled=True)
    return pairs.reshape(CHIPS * rows, HD)


def local(query, key, value, query_t, key_t, value_t, query_gain, key_gain):
    place = lax.axis_index("z") * 2 + lax.axis_index("ylo")
    share = lax.axis_index("yhi") * 2 + lax.axis_index("core")
    first = (place * ROWS + share * LOCAL).reshape(1)
    rows = [a.reshape(LOCAL, D) for a in (query, key, value, query_t, key_t, value_t)]
    landing = [pltpu.VMEM((LOCAL, D), BF16)] * 6 + [pltpu.VMEM((1, HD), F32)] * 2
    landing.append(pltpu.SemaphoreType.DMA((8,)))
    message = call(
        prepare,
        [((CHIPS * SEND, HD), BF16)],
        landing,
        specs=[SMEM] + [HBM] * 8,
    )(first, *rows, query_gain.reshape(1, HD), key_gain.reshape(1, HD))
    received = exchanged(message, SEND)
    query_pair, own = call(repack, [((QUERIES, 2 * HD), BF16), ((KEYS, 4 * HD), BF16)])(received)
    beside = lax.ppermute(own, "core", [(0, 1), (1, 0)])
    state_shapes = [((QUERIES, 1), F32)] * 3 + [((QUERIES, HD), F32)] * 2
    state = call(attend_first, state_shapes, keys=KEYS)(query_pair, own)
    message = call(
        attend_last, [((CHIPS * BACK, HD), BF16)], [pltpu.VMEM((QUERIES, HD), F32)] * 2, keys=KEYS
    )(query_pair, beside, *state)
    received = exchanged(message, BACK)
    attended, attended_t = call(unpack, [((LOCAL, D), BF16)] * 2, kept=False)(received)
    return attended.reshape(1, LOCAL, D), attended_t.reshape(1, LOCAL, D)


def solution(mesh):
    fine = Mesh(mesh.devices.reshape(4, 2, 8, 2, 4), ("yhi", "core", "z", "ylo", "x"))
    spec = P(("z", "ylo", "x"), ("yhi", "core"), None)
    return jax.shard_map(
        local,
        mesh=fine,
        in_specs=(spec,) * 6 + (P(), P()),
        out_specs=(spec, spec),
        check_vma=False,
    )
```

time: 92.5 us -> 88.5 us (0.957)
  blocking collectives: 79.8 us -> 76.3 us
    all_to_all x2, blocking collectives: 79.8 us -> 76.3 us  [exchanged(): pairs = lax.all_to_all(pairs, ('yhi', 'z', 'ylo'), 0, 0, tiled=True)]
  transfers between devices with their start and end apart: 1 -> 1, of which waited for: 1 -> 1; matrix products, arithmetic and copies ran while one was open for 0% -> 0% of each run, Pallas kernels for 2% -> 3%
where the time goes in v5:
time: 88.5 us; the launch traced here: 88.2 us
  blocking collectives  76.3 us (86%)
  Pallas kernels  8.78 us (10%)
  starting transfers between devices  1.92 us (2%)
    all_to_all x2, blocking collectives, exchanged(): pairs = lax.all_to_all(pairs, ('yhi', 'z', 'ylo'), 0, 0, tiled=True)  76.3 us
    pallas_call x5, Pallas kernels, run(): pl.pallas_call(kernel, out_shape=shapes[0] if one else shapes, in_specs=p...  8.78 us
    ppermute x1, starting transfers between devices, local(): beside = lax.ppermute(own, 'core', [(0, 1), (1, 0)])  1.92 us
  transfers between devices with their start and end apart: 1, of which 1 were waited for; matrix products, arithmetic and copies ran while one was open for 0% of the time, Pallas kernels for 3%

profile of v5, /device:TPU:6, one launch (start us, length us, event | category | flops | bytes accessed | tf_op | source)
XLA Modules:
  0.0 88.2 jit_solution(7559471112961180461)
XLA Ops:
  0.6 2.4 %prepare.1 = bf16[5760,128]{1,0:T(8,128)(2,1)S(1)} custom-call(s32[1]{0:T(128)} %bitcast.first, bf16[18,3072]{1,0:T(8,128)(2,1)} %bitcast.19, bf16[18,3072]{1,0:T(8,128)(2,1)} %bitcast.20, bf16[18,3072]{1,0:T(8,128)(2,1)} %bitcast.21, bf16[18,3072]{1,0:T(8,128)(2,1)} %bitcast.22, bf16[18,3072]{1,0:T(8,128)(2,1)} %bitcast.23, bf16[18,3072]{1,0:T(8,128)(2,1)} %bitcast.24, ...), custom_call_target="tpu_custom_call" | custom-call | bytes 1000000 | tf_op jit(solution)/shard_map/prepare/pallas_call | solution.py:195
  3.0 53.8 %all_to_all.10 = bf16[64,45,2,128]{3,2,1,0:T(2,128)(2,1)S(1)} all-to-all(bf16[64,45,2,128]{3,2,1,0:T(2,128)(2,1)S(1)} %bitcast.15), channel_id=1, replica_groups=mesh['yhi'=4,'core'=2,'z'=8,'ylo'=2,'x'=4] {'yhi','z','ylo'}, dimensions={0} | all-to-all | bytes 2949120 | tf_op jit(solution)/shard_map/all_to_all | solution.py:213
  56.9 0.5 repack.1
  57.4 1.9 %collective-permute-start = (bf16[1152,512]{1,0:T(8,128)(2,1)S(1)}, bf16[1152,512]{1,0:T(8,128)(2,1)S(1)}, u32[]{:S(2)}, u32[]{:S(2)}) collective-permute-start(bf16[1152,512]{1,0:T(8,128)(2,1)S(1)} %get-tuple-element.12.rest_0_), channel_id=1, source_target_pairs={{0,64},{64,0},{1,65},{65,1},{2,66},{66,2},{3,67},{67,3},{4,68},{68... | collective-permute-start | bytes 3538952 | tf_op jit(solution)/shard_map/ppermute | solution.py:232
  59.3 2.3 %attend_first.1 = (f32[576,1]{1,0:T(8,128)S(1)}, f32[576,1]{1,0:T(8,128)S(1)}, f32[576,1]{1,0:T(8,128)S(1)}, f32[576,128]{1,0:T(8,128)S(1)}, f32[576,128]{1,0:T(8,128)S(1)}) custom-call(bf16[576,256]{1,0:T(8,128)(2,1)S(1)} %get-tuple-element.11.query_pair, bf16[1152,512]{1,0:T(8,128)(2,1)S(1)} %get-tuple-element.12.rest_0_), custom_call_target="tpu_custom_call" | custom-call | flops 1358954496 | bytes 1000000 | tf_op jit(solution)/shard_map/attend_first/pallas_call | solution.py:195
  61.6 0.5 collective-permute-done.kv
  62.1 2.8 %attend_last.1 = bf16[1152,128]{1,0:T(8,128)(2,1)S(1)} custom-call(bf16[576,256]{1,0:T(8,128)(2,1)S(1)} %get-tuple-element.11.query_pair, bf16[1152,512]{1,0:T(8,128)(2,1)S(1)} %collective-permute-done.kv, f32[576,1]{1,0:T(8,128)S(1)} %get-tuple-element.13.rest_0_, f32[576,1]{1,0:T(8,128)S(1)} %get-tuple-element.14.rest_1_, ...), custom_call_target="tpu_custom_call" | custom-call | flops 1358954496 | bytes 1000000 | tf_op jit(solution)/shard_map/attend_last/pallas_call | solution.py:195
  64.9 22.5 %all_to_all.11 = bf16[64,9,2,128]{3,2,1,0:T(2,128)(2,1)S(1)} all-to-all(bf16[64,9,2,128]{3,2,1,0:T(2,128)(2,1)S(1)} %bitcast.18), channel_id=1, replica_groups=mesh['yhi'=4,'core'=2,'z'=8,'ylo'=2,'x'=4] {'yhi','z','ylo'}, dimensions={0} | all-to-all | bytes 589824 | tf_op jit(solution)/shard_map/all_to_all | solution.py:213
  87.4 0.8 unpack.1
Async XLA Ops:
  57.4 4.7 %collective-permute-start = (bf16[1152,512]{1,0:T(8,128)(2,1)S(1)}, bf16[1152,512]{1,0:T(8,128)(2,1)S(1)}, u32[]{:S(2)}, u32[]{:S(2)}) collective-permute-start(bf16[1152,512]{1,0:T(8,128)(2,1)S(1)} %get-tuple-element.12.rest_0_), channel_id=1, source_target_pairs={{0,64},{64,0},{1,65},{65,1},{2,66},{66,2},{3,67},{67,3},{4,68},{68... | collective-permute-start | bytes 3538952 | tf_op jit(solution)/shard_map/ppermute | solution.py:232

commit v6 on v5

--- a/solution.py
+++ b/solution.py
@@ -103,13 +103,16 @@
             out[at + 4 * LOCAL : at + SEND, :] = queries.astype(BF16)
 
 
-def repack(received, query_pair, own):
+def repack_keys(received, keys):
     for source in range(CHIPS):
         at = source * SEND
         for t in range(4):
-            own[LOCAL * source : LOCAL * source + LOCAL, HD * t : HD * t + HD] = received[
+            keys[LOCAL * source : LOCAL * source + LOCAL, HD * t : HD * t + HD] = received[
                 at + LOCAL * t : at + LOCAL * t + LOCAL, :
             ]
+
+
+def repack_queries(received, query_pair):
     for source in range(0, CHIPS, 2):
         two = [received[s * SEND + 4 * LOCAL : s * SEND + SEND, :].astype(F32) for s in (source, source + 1)]
         rows = slice(HALF * source, HALF * source + LOCAL)
@@ -118,7 +121,7 @@
 
 
 TRANSPOSED = (((1,), (1,)), ((), ()))
-BQ = 192
+BQ = 576
 
 
 def absorb(query_pair, blocks, at, state):
@@ -150,15 +153,18 @@
 QUERY_BLOCKS = [slice(b, b + BQ) for b in range(0, QUERIES, BQ)]
 
 
-def attend_first(query_pair, *rest):
-    blocks, state = rest[:-5], rest[-5:]
+def attend_first(received, query_pair, *rest):
+    state, keys = rest[:-1], rest[-1]
+    repack_queries(received, query_pair)
+    repack_keys(received, keys)
     for at in QUERY_BLOCKS:
-        for ref, part in zip(state, absorb(query_pair, blocks, at, None)):
+        for ref, part in zip(state, absorb(query_pair, (keys,), at, None)):
             ref[at, :] = part
 
 
-def attend_last(query_pair, kv, *rest):
-    before, (out, attended, attended_t) = rest[:5], rest[5:]
+def attend_last(query_pair, received, *rest):
+    before, (out, kv, attended, attended_t) = rest[:5], rest[5:]
+    repack_keys(received, kv)
     for at in QUERY_BLOCKS:
         state = absorb(query_pair, (kv,), at, [ref[at, :] for ref in before])
         _, total, drift, summed, summed_dot = state
@@ -228,12 +234,15 @@
         specs=[SMEM] + [HBM] * 8,
     )(first, *rows, query_gain.reshape(1, HD), key_gain.reshape(1, HD))
     received = exchanged(message, SEND)
-    query_pair, own = call(repack, [((QUERIES, 2 * HD), BF16), ((KEYS, 4 * HD), BF16)])(received)
-    beside = lax.ppermute(own, "core", [(0, 1), (1, 0)])
+    beside = lax.ppermute(received, "core", [(0, 1), (1, 0)])
     state_shapes = [((QUERIES, 1), F32)] * 3 + [((QUERIES, HD), F32)] * 2
-    state = call(attend_first, state_shapes, keys=KEYS)(query_pair, own)
+    keys = pltpu.VMEM((KEYS, 4 * HD), BF16)
+    query_pair, *state = call(attend_first, [((QUERIES, 2 * HD), BF16)] + state_shapes, [keys], keys=KEYS)(received)
     message = call(
-        attend_last, [((CHIPS * BACK, HD), BF16)], [pltpu.VMEM((QUERIES, HD), F32)] * 2, keys=KEYS
+        attend_last,
+        [((CHIPS * BACK, HD), BF16)],
+        [keys] + [pltpu.VMEM((QUERIES, HD), F32)] * 2,
+        keys=KEYS,
     )(query_pair, beside, *state)
     received = exchanged(message, BACK)
     attended, attended_t = call(unpack, [((LOCAL, D), BF16)] * 2, kept=False)(received)

time: 88.5 us -> 88.1 us (level)
    pallas_call x5 -> x4, Pallas kernels: 8.78 us -> 8.13 us  [run(): pl.pallas_call(kernel, out_shape=shapes[0] if one else shapes, in_specs=p...]
where the time goes in v6:
time: 88.1 us; the launch traced here: 87.9 us
  blocking collectives  76.3 us (87%)
  Pallas kernels  8.13 us (9%)
  starting transfers between devices  1.91 us (2%)
    all_to_all x2, blocking collectives, exchanged(): pairs = lax.all_to_all(pairs, ('yhi', 'z', 'ylo'), 0, 0, tiled=True)  76.3 us
    pallas_call x4, Pallas kernels, run(): pl.pallas_call(kernel, out_shape=shapes[0] if one else shapes, in_specs=p...  8.13 us
    ppermute x1, starting transfers between devices, local(): beside = lax.ppermute(received, 'core', [(0, 1), (1, 0)])  1.91 us
  transfers between devices with their start and end apart: 1, of which 1 were waited for; matrix products, arithmetic and copies ran while one was open for 0% of the time, Pallas kernels for 3%

profile of v6, /device:TPU:6, one launch (start us, length us, event | category | flops | bytes accessed | tf_op | source)
XLA Modules:
  0.0 87.9 jit_solution(15081326570729204215)
XLA Ops:
  0.6 2.4 %prepare.1 = bf16[5760,128]{1,0:T(8,128)(2,1)S(1)} custom-call(s32[1]{0:T(128)} %bitcast.first, bf16[18,3072]{1,0:T(8,128)(2,1)} %bitcast.20, bf16[18,3072]{1,0:T(8,128)(2,1)} %bitcast.21, bf16[18,3072]{1,0:T(8,128)(2,1)} %bitcast.22, bf16[18,3072]{1,0:T(8,128)(2,1)} %bitcast.23, bf16[18,3072]{1,0:T(8,128)(2,1)} %bitcast.24, bf16[18,3072]{1,0:T(8,128)(2,1)} %bitcast.25, ...), custom_call_target="tpu_custom_call" | custom-call | bytes 1000000 | tf_op jit(solution)/shard_map/prepare/pallas_call | solution.py:201
  3.0 53.8 %all_to_all.10 = bf16[64,45,2,128]{3,2,1,0:T(2,128)(2,1)S(1)} all-to-all(bf16[64,45,2,128]{3,2,1,0:T(2,128)(2,1)S(1)} %bitcast.15), channel_id=1, replica_groups=mesh['yhi'=4,'core'=2,'z'=8,'ylo'=2,'x'=4] {'yhi','z','ylo'}, dimensions={0} | all-to-all | bytes 2949120 | tf_op jit(solution)/shard_map/all_to_all | solution.py:219
  56.9 1.9 %collective-permute-start = (bf16[5760,128]{1,0:T(8,128)(2,1)S(1)}, bf16[5760,128]{1,0:T(8,128)(2,1)S(1)}, u32[]{:S(2)}, u32[]{:S(2)}) collective-permute-start(bf16[5760,128]{1,0:T(8,128)(2,1)S(1)} %bitcast.16), channel_id=1, source_target_pairs={{0,64},{64,0},{1,65},{65,1},{2,66},{66,2},{3,67},{67,3},{4,68},{68... | collective-permute-start | bytes 4423688 | tf_op jit(solution)/shard_map/ppermute | solution.py:237
  58.8 2.4 %attend_first.1 = (bf16[576,256]{1,0:T(8,128)(2,1)S(1)}, f32[576,1]{1,0:T(8,128)S(1)}, f32[576,1]{1,0:T(8,128)S(1)}, f32[576,1]{1,0:T(8,128)S(1)}, f32[576,128]{1,0:T(8,128)S(1)}, /*index=5*/f32[576,128]{1,0:T(8,128)S(1)}) custom-call(bf16[5760,128]{1,0:T(8,128)(2,1)S(1)} %bitcast.17), custom_call_target="tpu_custom_call" | custom-call | flops 1358954496 | bytes 1000000 | tf_op jit(solution)/shard_map/attend_first/pallas_call | solution.py:201
  61.2 0.9 collective-permute-done.received
  62.0 2.6 %attend_last.1 = bf16[1152,128]{1,0:T(8,128)(2,1)S(1)} custom-call(bf16[576,256]{1,0:T(8,128)(2,1)S(1)} %get-tuple-element.10.query_pair, bf16[5760,128]{1,0:T(8,128)(2,1)S(1)} %collective-permute-done.received, f32[576,1]{1,0:T(8,128)S(1)} %get-tuple-element.11.rest_0_, f32[576,1]{1,0:T(8,128)S(1)} %get-tuple-element.12.rest_1_, ...), custom_call_target="tpu_custom_call" | custom-call | flops 1358954496 | bytes 1000000 | tf_op jit(solution)/shard_map/attend_last/pallas_call | solution.py:201
  64.6 22.5 %all_to_all.11 = bf16[64,9,2,128]{3,2,1,0:T(2,128)(2,1)S(1)} all-to-all(bf16[64,9,2,128]{3,2,1,0:T(2,128)(2,1)S(1)} %bitcast.19), channel_id=1, replica_groups=mesh['yhi'=4,'core'=2,'z'=8,'ylo'=2,'x'=4] {'yhi','z','ylo'}, dimensions={0} | all-to-all | bytes 589824 | tf_op jit(solution)/shard_map/all_to_all | solution.py:219
  87.1 0.8 unpack.1
Async XLA Ops:
  56.9 5.2 %collective-permute-start = (bf16[5760,128]{1,0:T(8,128)(2,1)S(1)}, bf16[5760,128]{1,0:T(8,128)(2,1)S(1)}, u32[]{:S(2)}, u32[]{:S(2)}) collective-permute-start(bf16[5760,128]{1,0:T(8,128)(2,1)S(1)} %bitcast.16), channel_id=1, source_target_pairs={{0,64},{64,0},{1,65},{65,1},{2,66},{66,2},{3,67},{67,3},{4,68},{68... | collective-permute-start | bytes 4423688 | tf_op jit(solution)/shard_map/ppermute | solution.py:237

commit v7 on v5

--- a/solution.py
+++ b/solution.py
@@ -103,13 +103,16 @@
             out[at + 4 * LOCAL : at + SEND, :] = queries.astype(BF16)
 
 
-def repack(received, query_pair, own):
+def repack_keys(received, keys):
     for source in range(CHIPS):
         at = source * SEND
         for t in range(4):
-            own[LOCAL * source : LOCAL * source + LOCAL, HD * t : HD * t + HD] = received[
+            keys[LOCAL * source : LOCAL * source + LOCAL, HD * t : HD * t + HD] = received[
                 at + LOCAL * t : at + LOCAL * t + LOCAL, :
             ]
+
+
+def repack_queries(received, query_pair):
     for source in range(0, CHIPS, 2):
         two = [received[s * SEND + 4 * LOCAL : s * SEND + SEND, :].astype(F32) for s in (source, source + 1)]
         rows = slice(HALF * source, HALF * source + LOCAL)
@@ -118,7 +121,7 @@
 
 
 TRANSPOSED = (((1,), (1,)), ((), ()))
-BQ = 192
+BQ = 576
 
 
 def absorb(query_pair, blocks, at, state):
@@ -150,10 +153,10 @@
 QUERY_BLOCKS = [slice(b, b + BQ) for b in range(0, QUERIES, BQ)]
 
 
-def attend_first(query_pair, *rest):
-    blocks, state = rest[:-5], rest[-5:]
+def attend_first(received, keys, query_pair, *state):
+    repack_queries(received, query_pair)
     for at in QUERY_BLOCKS:
-        for ref, part in zip(state, absorb(query_pair, blocks, at, None)):
+        for ref, part in zip(state, absorb(query_pair, (keys,), at, None)):
             ref[at, :] = part
 
 
@@ -228,10 +231,10 @@
         specs=[SMEM] + [HBM] * 8,
     )(first, *rows, query_gain.reshape(1, HD), key_gain.reshape(1, HD))
     received = exchanged(message, SEND)
-    query_pair, own = call(repack, [((QUERIES, 2 * HD), BF16), ((KEYS, 4 * HD), BF16)])(received)
-    beside = lax.ppermute(own, "core", [(0, 1), (1, 0)])
+    keys = call(repack_keys, [((KEYS, 4 * HD), BF16)])(received)
+    beside = lax.ppermute(keys, "core", [(0, 1), (1, 0)])
     state_shapes = [((QUERIES, 1), F32)] * 3 + [((QUERIES, HD), F32)] * 2
-    state = call(attend_first, state_shapes, keys=KEYS)(query_pair, own)
+    query_pair, *state = call(attend_first, [((QUERIES, 2 * HD), BF16)] + state_shapes, keys=KEYS)(received, keys)
     message = call(
         attend_last, [((CHIPS * BACK, HD), BF16)], [pltpu.VMEM((QUERIES, HD), F32)] * 2, keys=KEYS
     )(query_pair, beside, *state)

time: 88.5 us -> 87.9 us (level)
  transfers between devices with their start and end apart: 1 -> 1, of which waited for: 1 -> 1; matrix products, arithmetic and copies ran while one was open for 0% -> 0% of each run, Pallas kernels for 3% -> 2%
where the time goes in v7:
time: 87.9 us; the launch traced here: 87.7 us
  blocking collectives  76.3 us (87%)
  Pallas kernels  8.03 us (9%)
  starting transfers between devices  1.92 us (2%)
    all_to_all x2, blocking collectives, exchanged(): pairs = lax.all_to_all(pairs, ('yhi', 'z', 'ylo'), 0, 0, tiled=True)  76.3 us
    pallas_call x5, Pallas kernels, run(): pl.pallas_call(kernel, out_shape=shapes[0] if one else shapes, in_specs=p...  8.03 us
    ppermute x1, starting transfers between devices, local(): beside = lax.ppermute(keys, 'core', [(0, 1), (1, 0)])  1.92 us
  transfers between devices with their start and end apart: 1, of which 1 were waited for; matrix products, arithmetic and copies ran while one was open for 0% of the time, Pallas kernels for 2%

profile of v7, /device:TPU:6, one launch (start us, length us, event | category | flops | bytes accessed | tf_op | source)
XLA Modules:
  0.0 87.7 jit_solution(8123810187916154631)
XLA Ops:
  0.6 2.4 %prepare.1 = bf16[5760,128]{1,0:T(8,128)(2,1)S(1)} custom-call(s32[1]{0:T(128)} %bitcast.first, bf16[18,3072]{1,0:T(8,128)(2,1)} %bitcast.20, bf16[18,3072]{1,0:T(8,128)(2,1)} %bitcast.21, bf16[18,3072]{1,0:T(8,128)(2,1)} %bitcast.22, bf16[18,3072]{1,0:T(8,128)(2,1)} %bitcast.23, bf16[18,3072]{1,0:T(8,128)(2,1)} %bitcast.24, bf16[18,3072]{1,0:T(8,128)(2,1)} %bitcast.25, ...), custom_call_target="tpu_custom_call" | custom-call | bytes 1000000 | tf_op jit(solution)/shard_map/prepare/pallas_call | solution.py:198
  3.0 53.8 %all_to_all.10 = bf16[64,45,2,128]{3,2,1,0:T(2,128)(2,1)S(1)} all-to-all(bf16[64,45,2,128]{3,2,1,0:T(2,128)(2,1)S(1)} %bitcast.15), channel_id=1, replica_groups=mesh['yhi'=4,'core'=2,'z'=8,'ylo'=2,'x'=4] {'yhi','z','ylo'}, dimensions={0} | all-to-all | bytes 2949120 | tf_op jit(solution)/shard_map/all_to_all | solution.py:216
  56.9 0.4 repack_keys.1.keys
  57.2 1.9 %collective-permute-start = (bf16[1152,512]{1,0:T(8,128)(2,1)S(1)}, bf16[1152,512]{1,0:T(8,128)(2,1)S(1)}, u32[]{:S(2)}, u32[]{:S(2)}) collective-permute-start(bf16[1152,512]{1,0:T(8,128)(2,1)S(1)} %repack_keys.1.keys), channel_id=1, source_target_pairs={{0,64},{64,0},{1,65},{65,1},{2,66},{66,2},{3,67},{67,3},{4,68},{68... | collective-permute-start | bytes 3538952 | tf_op jit(solution)/shard_map/ppermute | solution.py:235
  59.2 2.1 %attend_first.1 = (bf16[576,256]{1,0:T(8,128)(2,1)S(1)}, f32[576,1]{1,0:T(8,128)S(1)}, f32[576,1]{1,0:T(8,128)S(1)}, f32[576,1]{1,0:T(8,128)S(1)}, f32[576,128]{1,0:T(8,128)S(1)}, /*index=5*/f32[576,128]{1,0:T(8,128)S(1)}) custom-call(bf16[5760,128]{1,0:T(8,128)(2,1)S(1)} %bitcast.17, bf16[1152,512]{1,0:T(8,128)(2,1)S(1)} %repack_keys.1.keys), custom_call_target="tpu_custom_call" | custom-call | flops 1358954496 | bytes 1000000 | tf_op jit(solution)/shard_map/attend_first/pallas_call | solution.py:198
  61.3 0.7 collective-permute-done.kv
  62.0 2.4 %attend_last.1 = bf16[1152,128]{1,0:T(8,128)(2,1)S(1)} custom-call(bf16[576,256]{1,0:T(8,128)(2,1)S(1)} %get-tuple-element.10.query_pair, bf16[1152,512]{1,0:T(8,128)(2,1)S(1)} %collective-permute-done.kv, f32[576,1]{1,0:T(8,128)S(1)} %get-tuple-element.11.rest_0_, f32[576,1]{1,0:T(8,128)S(1)} %get-tuple-element.12.rest_1_, ...), custom_call_target="tpu_custom_call" | custom-call | flops 1358954496 | bytes 1000000 | tf_op jit(solution)/shard_map/attend_last/pallas_call | solution.py:198
  64.4 22.5 %all_to_all.11 = bf16[64,9,2,128]{3,2,1,0:T(2,128)(2,1)S(1)} all-to-all(bf16[64,9,2,128]{3,2,1,0:T(2,128)(2,1)S(1)} %bitcast.19), channel_id=1, replica_groups=mesh['yhi'=4,'core'=2,'z'=8,'ylo'=2,'x'=4] {'yhi','z','ylo'}, dimensions={0} | all-to-all | bytes 589824 | tf_op jit(solution)/shard_map/all_to_all | solution.py:216
  86.9 0.8 unpack.1
Async XLA Ops:
  57.2 4.7 %collective-permute-start = (bf16[1152,512]{1,0:T(8,128)(2,1)S(1)}, bf16[1152,512]{1,0:T(8,128)(2,1)S(1)}, u32[]{:S(2)}, u32[]{:S(2)}) collective-permute-start(bf16[1152,512]{1,0:T(8,128)(2,1)S(1)} %repack_keys.1.keys), channel_id=1, source_target_pairs={{0,64},{64,0},{1,65},{65,1},{2,66},{66,2},{3,67},{67,3},{4,68},{68... | collective-permute-start | bytes 3538952 | tf_op jit(solution)/shard_map/ppermute | solution.py:235

commit v8 on v7

--- a/solution.py
+++ b/solution.py
@@ -46,8 +46,8 @@
         pltpu.make_async_copy(source, buffer, arrival.at[i])
         for i, (source, buffer) in enumerate(zip(sources, buffers))
     ]
-    for copy in copies:
-        copy.start()
+    for i in (6, 7, 0, 3, 1, 4, 2, 5):
+        copies[i].start()
     query, key, value, query_t, key_t, value_t, query_gain, key_gain = buffers
     token = first[0] + lax.broadcasted_iota(jnp.int32, (LOCAL, HD), 0)
     lane = lax.broadcasted_iota(jnp.int32, (LOCAL, HD), 1)
@@ -85,22 +85,28 @@
 
     idle = 2 * HEADS * SEND
     out[idle:, :] = jnp.zeros((CHIPS * SEND - idle, HD), BF16)
-    for copy in copies:
-        copy.wait()
+    for i in (6, 7, 0, 3):
+        copies[i].wait()
     of_query = turned(query_gain[...])
     of_key = turned(key_gain[...])
     for head in range(HEADS):
         here = lanes(head)
         q_hat, q_dot = normalize(query[:, here], query_t[:, here], *of_query)
+        for half in range(2):
+            at = chip_of(head, half) * SEND
+            ours = slice(HALF * half, HALF * half + HALF)
+            queries = jnp.concatenate([q_hat[ours], q_dot[ours]], axis=0)
+            out[at + 4 * LOCAL : at + SEND, :] = queries.astype(BF16)
+    for i in (1, 4, 2, 5):
+        copies[i].wait()
+    for head in range(HEADS):
+        here = lanes(head)
         k_hat, k_dot = normalize(key[:, here], key_t[:, here], *of_key)
         parts = (k_hat.astype(BF16), k_dot.astype(BF16), value[:, here], value_t[:, here])
         for half in range(2):
             at = chip_of(head, half) * SEND
             for t, part in enumerate(parts):
                 out[at + LOCAL * t : at + LOCAL * t + LOCAL, :] = part
-            ours = slice(HALF * half, HALF * half + HALF)
-            queries = jnp.concatenate([q_hat[ours], q_dot[ours]], axis=0)
-            out[at + 4 * LOCAL : at + SEND, :] = queries.astype(BF16)
 
 
 def repack_keys(received, keys):
@@ -136,13 +142,14 @@
     for s, kv in zip(scores, blocks):
         weights = jnp.exp2((s - peak) * (SCALE * math.log2(math.e)))
         moved = lax.dot_general(pair, kv[:, 0 : 2 * HD], TRANSPOSED, preferred_element_type=F32)
-        product = weights * (moved * SCALE)
+        product = weights * moved
         total = total + jnp.sum(weights, axis=1, keepdims=True)
         drift = drift + jnp.sum(product, axis=1, keepdims=True)
         both = both + jnp.dot(weights.astype(BF16), kv[:, 2 * HD : 4 * HD], preferred_element_type=F32)
         extra = extra + jnp.dot(product.astype(BF16), kv[:, 2 * HD : 3 * HD], preferred_element_type=F32)
+    drift = drift * SCALE
     summed = both[:, :HD]
-    summed_dot = both[:, HD:] + extra
+    summed_dot = both[:, HD:] + extra * SCALE
     if state is None:
         return peak, total, drift, summed, summed_dot
     rescale = jnp.exp2((state[0] - peak) * (SCALE * math.log2(math.e)))

time: 87.9 us -> 87.7 us (level)
  no operation moved by 1% of the time
where the time goes in v8:
time: 87.7 us; the launch traced here: 87.5 us
  blocking collectives  76.3 us (87%)
  Pallas kernels  7.8 us (9%)
  starting transfers between devices  1.92 us (2%)
    all_to_all x2, blocking collectives, exchanged(): pairs = lax.all_to_all(pairs, ('yhi', 'z', 'ylo'), 0, 0, tiled=True)  76.3 us
    pallas_call x5, Pallas kernels, run(): pl.pallas_call(kernel, out_shape=shapes[0] if one else shapes, in_specs=p...  7.8 us
    ppermute x1, starting transfers between devices, local(): beside = lax.ppermute(keys, 'core', [(0, 1), (1, 0)])  1.92 us
  transfers between devices with their start and end apart: 1, of which 1 were waited for; matrix products, arithmetic and copies ran while one was open for 0% of the time, Pallas kernels for 2%

profile of v8, /device:TPU:6, one launch (start us, length us, event | category | flops | bytes accessed | tf_op | source)
XLA Modules:
  0.0 87.5 jit_solution(16157380713259927857)
XLA Ops:
  0.6 2.3 %prepare.1 = bf16[5760,128]{1,0:T(8,128)(2,1)S(1)} custom-call(s32[1]{0:T(128)} %bitcast.first, bf16[18,3072]{1,0:T(8,128)(2,1)} %bitcast.20, bf16[18,3072]{1,0:T(8,128)(2,1)} %bitcast.21, bf16[18,3072]{1,0:T(8,128)(2,1)} %bitcast.22, bf16[18,3072]{1,0:T(8,128)(2,1)} %bitcast.23, bf16[18,3072]{1,0:T(8,128)(2,1)} %bitcast.24, bf16[18,3072]{1,0:T(8,128)(2,1)} %bitcast.25, ...), custom_call_target="tpu_custom_call" | custom-call | bytes 1000000 | tf_op jit(solution)/shard_map/prepare/pallas_call | solution.py:205
  2.9 53.8 %all_to_all.10 = bf16[64,45,2,128]{3,2,1,0:T(2,128)(2,1)S(1)} all-to-all(bf16[64,45,2,128]{3,2,1,0:T(2,128)(2,1)S(1)} %bitcast.15), channel_id=1, replica_groups=mesh['yhi'=4,'core'=2,'z'=8,'ylo'=2,'x'=4] {'yhi','z','ylo'}, dimensions={0} | all-to-all | bytes 2949120 | tf_op jit(solution)/shard_map/all_to_all | solution.py:223
  56.8 0.4 repack_keys.1.keys
  57.1 1.9 %collective-permute-start = (bf16[1152,512]{1,0:T(8,128)(2,1)S(1)}, bf16[1152,512]{1,0:T(8,128)(2,1)S(1)}, u32[]{:S(2)}, u32[]{:S(2)}) collective-permute-start(bf16[1152,512]{1,0:T(8,128)(2,1)S(1)} %repack_keys.1.keys), channel_id=1, source_target_pairs={{0,64},{64,0},{1,65},{65,1},{2,66},{66,2},{3,67},{67,3},{4,68},{68... | collective-permute-start | bytes 3538952 | tf_op jit(solution)/shard_map/ppermute | solution.py:242
  59.1 2.1 %attend_first.1 = (bf16[576,256]{1,0:T(8,128)(2,1)S(1)}, f32[576,1]{1,0:T(8,128)S(1)}, f32[576,1]{1,0:T(8,128)S(1)}, f32[576,1]{1,0:T(8,128)S(1)}, f32[576,128]{1,0:T(8,128)S(1)}, /*index=5*/f32[576,128]{1,0:T(8,128)S(1)}) custom-call(bf16[5760,128]{1,0:T(8,128)(2,1)S(1)} %bitcast.17, bf16[1152,512]{1,0:T(8,128)(2,1)S(1)} %repack_keys.1.keys), custom_call_target="tpu_custom_call" | custom-call | flops 1358954496 | bytes 1000000 | tf_op jit(solution)/shard_map/attend_first/pallas_call | solution.py:205
  61.1 0.8 collective-permute-done.kv
  61.9 2.3 %attend_last.1 = bf16[1152,128]{1,0:T(8,128)(2,1)S(1)} custom-call(bf16[576,256]{1,0:T(8,128)(2,1)S(1)} %get-tuple-element.10.query_pair, bf16[1152,512]{1,0:T(8,128)(2,1)S(1)} %collective-permute-done.kv, f32[576,1]{1,0:T(8,128)S(1)} %get-tuple-element.11.rest_0_, f32[576,1]{1,0:T(8,128)S(1)} %get-tuple-element.12.rest_1_, ...), custom_call_target="tpu_custom_call" | custom-call | flops 1358954496 | bytes 1000000 | tf_op jit(solution)/shard_map/attend_last/pallas_call | solution.py:205
  64.2 22.5 %all_to_all.11 = bf16[64,9,2,128]{3,2,1,0:T(2,128)(2,1)S(1)} all-to-all(bf16[64,9,2,128]{3,2,1,0:T(2,128)(2,1)S(1)} %bitcast.19), channel_id=1, replica_groups=mesh['yhi'=4,'core'=2,'z'=8,'ylo'=2,'x'=4] {'yhi','z','ylo'}, dimensions={0} | all-to-all | bytes 589824 | tf_op jit(solution)/shard_map/all_to_all | solution.py:223
  86.7 0.8 unpack.1
Async XLA Ops:
  57.1 4.7 %collective-permute-start = (bf16[1152,512]{1,0:T(8,128)(2,1)S(1)}, bf16[1152,512]{1,0:T(8,128)(2,1)S(1)}, u32[]{:S(2)}, u32[]{:S(2)}) collective-permute-start(bf16[1152,512]{1,0:T(8,128)(2,1)S(1)} %repack_keys.1.keys), channel_id=1, source_target_pairs={{0,64},{64,0},{1,65},{65,1},{2,66},{66,2},{3,67},{67,3},{4,68},{68... | collective-permute-start | bytes 3538952 | tf_op jit(solution)/shard_map/ppermute | solution.py:242

commit v9 on v8

--- a/solution.py
+++ b/solution.py
@@ -62,7 +62,7 @@
     angle = jnp.where(pair < 8, 0.0, jnp.where(of_row, row_id, column_id) * frequency)
     cosine = jnp.cos(angle)
     even = (lane & 1) == 0
-    sine = jnp.where(even, -jnp.sin(angle), jnp.sin(angle))
+    sine = jnp.sin(jnp.where(even, -angle, angle))
 
     def turned(gain):
         wide = jnp.broadcast_to(gain, (LOCAL, HD))
@@ -97,15 +97,22 @@
             ours = slice(HALF * half, HALF * half + HALF)
             queries = jnp.concatenate([q_hat[ours], q_dot[ours]], axis=0)
             out[at + 4 * LOCAL : at + SEND, :] = queries.astype(BF16)
-    for i in (1, 4, 2, 5):
+    for i in (1, 4):
         copies[i].wait()
     for head in range(HEADS):
         here = lanes(head)
-        k_hat, k_dot = normalize(key[:, here], key_t[:, here], *of_key)
-        parts = (k_hat.astype(BF16), k_dot.astype(BF16), value[:, here], value_t[:, here])
+        keys = normalize(key[:, here], key_t[:, here], *of_key)
         for half in range(2):
             at = chip_of(head, half) * SEND
-            for t, part in enumerate(parts):
+            for t, part in enumerate(keys):
+                out[at + LOCAL * t : at + LOCAL * t + LOCAL, :] = part.astype(BF16)
+    for i in (2, 5):
+        copies[i].wait()
+    for head in range(HEADS):
+        here = lanes(head)
+        for half in range(2):
+            at = chip_of(head, half) * SEND
+            for t, part in enumerate((value[:, here], value_t[:, here]), 2):
                 out[at + LOCAL * t : at + LOCAL * t + LOCAL, :] = part
 
 
@@ -142,14 +149,13 @@
     for s, kv in zip(scores, blocks):
         weights = jnp.exp2((s - peak) * (SCALE * math.log2(math.e)))
         moved = lax.dot_general(pair, kv[:, 0 : 2 * HD], TRANSPOSED, preferred_element_type=F32)
-        product = weights * moved
+        product = weights * (moved * SCALE)
         total = total + jnp.sum(weights, axis=1, keepdims=True)
         drift = drift + jnp.sum(product, axis=1, keepdims=True)
         both = both + jnp.dot(weights.astype(BF16), kv[:, 2 * HD : 4 * HD], preferred_element_type=F32)
         extra = extra + jnp.dot(product.astype(BF16), kv[:, 2 * HD : 3 * HD], preferred_element_type=F32)
-    drift = drift * SCALE
     summed = both[:, :HD]
-    summed_dot = both[:, HD:] + extra * SCALE
+    summed_dot = both[:, HD:] + extra
     if state is None:
         return peak, total, drift, summed, summed_dot
     rescale = jnp.exp2((state[0] - peak) * (SCALE * math.log2(math.e)))

time: 87.7 us -> 87.8 us (level)
  no operation moved by 1% of the time
where the time goes in v9:
time: 87.8 us; the launch traced here: 87.6 us
  blocking collectives  76.3 us (87%)
  Pallas kernels  7.93 us (9%)
  starting transfers between devices  1.92 us (2%)
    all_to_all x2, blocking collectives, exchanged(): pairs = lax.all_to_all(pairs, ('yhi', 'z', 'ylo'), 0, 0, tiled=True)  76.3 us
    pallas_call x5, Pallas kernels, run(): pl.pallas_call(kernel, out_shape=shapes[0] if one else shapes, in_specs=p...  7.93 us
    ppermute x1, starting transfers between devices, local(): beside = lax.ppermute(keys, 'core', [(0, 1), (1, 0)])  1.92 us
  transfers between devices with their start and end apart: 1, of which 1 were waited for; matrix products, arithmetic and copies ran while one was open for 0% of the time, Pallas kernels for 2%

profile of v9, /device:TPU:6, one launch (start us, length us, event | category | flops | bytes accessed | tf_op | source)
XLA Modules:
  0.0 87.6 jit_solution(17050904523883135462)
XLA Ops:
  0.6 2.3 %prepare.1 = bf16[5760,128]{1,0:T(8,128)(2,1)S(1)} custom-call(s32[1]{0:T(128)} %bitcast.first, bf16[18,3072]{1,0:T(8,128)(2,1)} %bitcast.20, bf16[18,3072]{1,0:T(8,128)(2,1)} %bitcast.21, bf16[18,3072]{1,0:T(8,128)(2,1)} %bitcast.22, bf16[18,3072]{1,0:T(8,128)(2,1)} %bitcast.23, bf16[18,3072]{1,0:T(8,128)(2,1)} %bitcast.24, bf16[18,3072]{1,0:T(8,128)(2,1)} %bitcast.25, ...), custom_call_target="tpu_custom_call" | custom-call | bytes 1000000 | tf_op jit(solution)/shard_map/prepare/pallas_call | solution.py:211
  2.9 53.8 %all_to_all.10 = bf16[64,45,2,128]{3,2,1,0:T(2,128)(2,1)S(1)} all-to-all(bf16[64,45,2,128]{3,2,1,0:T(2,128)(2,1)S(1)} %bitcast.15), channel_id=1, replica_groups=mesh['yhi'=4,'core'=2,'z'=8,'ylo'=2,'x'=4] {'yhi','z','ylo'}, dimensions={0} | all-to-all | bytes 2949120 | tf_op jit(solution)/shard_map/all_to_all | solution.py:229
  56.8 0.4 repack_keys.1.keys
  57.1 1.9 %collective-permute-start = (bf16[1152,512]{1,0:T(8,128)(2,1)S(1)}, bf16[1152,512]{1,0:T(8,128)(2,1)S(1)}, u32[]{:S(2)}, u32[]{:S(2)}) collective-permute-start(bf16[1152,512]{1,0:T(8,128)(2,1)S(1)} %repack_keys.1.keys), channel_id=1, source_target_pairs={{0,64},{64,0},{1,65},{65,1},{2,66},{66,2},{3,67},{67,3},{4,68},{68... | collective-permute-start | bytes 3538952 | tf_op jit(solution)/shard_map/ppermute | solution.py:248
  59.1 2.1 %attend_first.1 = (bf16[576,256]{1,0:T(8,128)(2,1)S(1)}, f32[576,1]{1,0:T(8,128)S(1)}, f32[576,1]{1,0:T(8,128)S(1)}, f32[576,1]{1,0:T(8,128)S(1)}, f32[576,128]{1,0:T(8,128)S(1)}, /*index=5*/f32[576,128]{1,0:T(8,128)S(1)}) custom-call(bf16[5760,128]{1,0:T(8,128)(2,1)S(1)} %bitcast.17, bf16[1152,512]{1,0:T(8,128)(2,1)S(1)} %repack_keys.1.keys), custom_call_target="tpu_custom_call" | custom-call | flops 1358954496 | bytes 1000000 | tf_op jit(solution)/shard_map/attend_first/pallas_call | solution.py:211
  61.2 0.7 collective-permute-done.kv
  61.9 2.4 %attend_last.1 = bf16[1152,128]{1,0:T(8,128)(2,1)S(1)} custom-call(bf16[576,256]{1,0:T(8,128)(2,1)S(1)} %get-tuple-element.10.query_pair, bf16[1152,512]{1,0:T(8,128)(2,1)S(1)} %collective-permute-done.kv, f32[576,1]{1,0:T(8,128)S(1)} %get-tuple-element.11.rest_0_, f32[576,1]{1,0:T(8,128)S(1)} %get-tuple-element.12.rest_1_, ...), custom_call_target="tpu_custom_call" | custom-call | flops 1358954496 | bytes 1000000 | tf_op jit(solution)/shard_map/attend_last/pallas_call | solution.py:211
  64.3 22.5 %all_to_all.11 = bf16[64,9,2,128]{3,2,1,0:T(2,128)(2,1)S(1)} all-to-all(bf16[64,9,2,128]{3,2,1,0:T(2,128)(2,1)S(1)} %bitcast.19), channel_id=1, replica_groups=mesh['yhi'=4,'core'=2,'z'=8,'ylo'=2,'x'=4] {'yhi','z','ylo'}, dimensions={0} | all-to-all | bytes 589824 | tf_op jit(solution)/shard_map/all_to_all | solution.py:229
  86.8 0.8 unpack.1
Async XLA Ops:
  57.1 4.7 %collective-permute-start = (bf16[1152,512]{1,0:T(8,128)(2,1)S(1)}, bf16[1152,512]{1,0:T(8,128)(2,1)S(1)}, u32[]{:S(2)}, u32[]{:S(2)}) collective-permute-start(bf16[1152,512]{1,0:T(8,128)(2,1)S(1)} %repack_keys.1.keys), channel_id=1, source_target_pairs={{0,64},{64,0},{1,65},{65,1},{2,66},{66,2},{3,67},{67,3},{4,68},{68... | collective-permute-start | bytes 3538952 | tf_op jit(solution)/shard_map/ppermute | solution.py:248
